TPU v7x, 16 devices: a whole 2x2x2 slice. The times are simulated.
16 devices in a mesh: ep: 16 (over z, y, x, core).
Axes of the slice: x: 2, y: 2, z: 2, core: 2. Of those that a mesh axis runs over, the one named last changes fastest.
Arguments:
- tokens: bfloat16 [128, 512, 768], P('ep')
- loss_weight: bfloat16 [128, 512, 768], P('ep')
- w_gate: bfloat16 [768, 64], replicated
- w_in: bfloat16 [64, 768, 3072], P('ep')
- w_out: bfloat16 [64, 3072, 768], P('ep')
- first_expert: int32 [128, 512], P('ep')
- second_expert: int32 [128, 512], P('ep')
- keep_second: int32 [128, 512], P('ep')
Outputs:
- output 1: float32 [], replicated
- output 2: bfloat16 [128, 512, 768], P('ep')
- output 3: bfloat16 [64, 768, 3072], P('ep')
- output 4: bfloat16 [64, 3072, 768], P('ep')
- output 5: float32 [768, 64], replicated
All inputs are finite; a program needn't handle non-finite values.
Results may differ from a plain program's by a relative error of at most 0.00960684.
Values are sent between devices in bfloat16 or wider.
A program may use at most 1 GiB of HBM per device.

v0:
```python
import jax
import jax.numpy as jnp
from jax import lax
from jax.sharding import PartitionSpec as P

ALPHA = 0.01


def gelu_bf16(pre_act):
    return jax.nn.gelu(pre_act, approximate=True).astype(jnp.bfloat16)


def route_masks(first_ids, second_ids, keep_ids, experts, cap_rows):
    seq_len = first_ids.shape[1]
    expert_ids = jnp.arange(experts, dtype=jnp.int32)
    first_hot = (first_ids[..., None] == expert_ids).astype(jnp.bfloat16)
    second_hot = (second_ids[..., None] == expert_ids).astype(jnp.bfloat16)
    second_kept = second_hot * keep_ids.astype(jnp.bfloat16)[..., None]
    seq_ids = jnp.arange(seq_len, dtype=jnp.int32)
    earlier = (seq_ids[:, None] > seq_ids[None, :]).astype(jnp.bfloat16)
    before_first = jnp.einsum('st,gte->gse', earlier, first_hot, preferred_element_type=jnp.float32)
    before_second = jnp.einsum('st,gte->gse', earlier, second_kept, preferred_element_type=jnp.float32)
    first_count = jnp.sum(first_hot, axis=1, dtype=jnp.float32)
    pos_first = jnp.sum(before_first * first_hot, axis=-1)
    pos_second = jnp.sum((before_second + first_count[:, None, :]) * second_hot, axis=-1)
    slot_ids = jnp.arange(cap_rows, dtype=jnp.float32)
    disp_first = first_hot[..., None] * (pos_first[..., None, None] == slot_ids).astype(jnp.bfloat16)
    disp_second = second_kept[..., None] * (pos_second[..., None, None] == slot_ids).astype(jnp.bfloat16)
    return first_hot, second_hot, first_count, disp_first, disp_second


def solution(mesh):
    ep_size = mesh.shape['ep']

    def layer_body(x_loc, r_loc, w_gate, w_in_loc, w_out_loc, first_ids, second_ids, keep_ids):
        local_groups, seq_len, hidden = x_loc.shape
        experts = w_gate.shape[1]
        cap_rows = 2 * seq_len // experts
        tokens_all = local_groups * ep_size * seq_len
        numel = tokens_all * hidden
        first_hot, second_hot, first_count, disp_first, disp_second = route_masks(first_ids, second_ids, keep_ids, experts, cap_rows)
        logits = jnp.einsum('gsh,he->gse', x_loc, w_gate, preferred_element_type=jnp.float32)
        router_prob = jax.nn.softmax(logits, axis=-1)
        gate_first = jnp.sum(router_prob * first_hot, axis=-1)
        gate_second = jnp.sum(router_prob * second_hot, axis=-1)
        gate_sum = gate_first + gate_second
        norm_first = (gate_first / gate_sum).astype(jnp.bfloat16)
        norm_second = (gate_second / gate_sum).astype(jnp.bfloat16)
        dispatch = disp_first + disp_second
        combine = disp_first * norm_first[..., None, None] + disp_second * norm_second[..., None, None]
        send_x = jnp.einsum('gsec,gsh->egch', dispatch, x_loc, preferred_element_type=jnp.float32).astype(jnp.bfloat16)
        expert_x = lax.all_to_all(send_x, 'ep', 0, 1, tiled=True)
        pre_act = jnp.einsum('egch,ehf->egcf', expert_x, w_in_loc, preferred_element_type=jnp.float32)
        act_bf, act_pull = jax.vjp(gelu_bf16, pre_act)
        expert_y = jnp.einsum('egcf,efh->egch', act_bf, w_out_loc, preferred_element_type=jnp.float32).astype(jnp.bfloat16)
        back_y = lax.all_to_all(expert_y, 'ep', 1, 0, tiled=True)
        out_first = jnp.einsum('gsec,egch->gsh', disp_first, back_y, preferred_element_type=jnp.float32).astype(jnp.bfloat16)
        out_second = jnp.einsum('gsec,egch->gsh', disp_second, back_y, preferred_element_type=jnp.float32).astype(jnp.bfloat16)
        moe_out = norm_first.astype(jnp.float32)[..., None] * out_first + norm_second.astype(jnp.float32)[..., None] * out_second
        dot_sum = jnp.einsum('gsh,gsh->', x_loc, r_loc, preferred_element_type=jnp.float32) + jnp.sum(moe_out * r_loc)
        local_stats = jnp.concatenate([jnp.sum(first_count, axis=0), jnp.sum(router_prob, axis=(0, 1)), dot_sum[None]])
        global_stats = lax.psum(local_stats, 'ep')
        frac_first = global_stats[:experts] / tokens_all
        mean_prob = global_stats[experts:2 * experts] / tokens_all
        loss_value = global_stats[2 * experts] / numel + ALPHA * experts * jnp.sum(frac_first * mean_prob)

        grad_send = jnp.einsum('gsec,gsh->egch', combine, r_loc, preferred_element_type=jnp.float32).astype(jnp.bfloat16)
        grad_y = lax.all_to_all(grad_send, 'ep', 0, 1, tiled=True)
        grad_w_out = jnp.einsum('egcf,egch->efh', act_bf, grad_y, preferred_element_type=jnp.float32).astype(jnp.bfloat16)
        grad_act = jnp.einsum('egch,efh->egcf', grad_y, w_out_loc, preferred_element_type=jnp.float32).astype(jnp.bfloat16)
        grad_pre = act_pull(grad_act)[0].astype(jnp.bfloat16)
        grad_w_in = jnp.einsum('egch,egcf->ehf', expert_x, grad_pre, preferred_element_type=jnp.float32).astype(jnp.bfloat16)
        grad_slots = jnp.einsum('egcf,ehf->egch', grad_pre, w_in_loc, preferred_element_type=jnp.float32).astype(jnp.bfloat16)
        grad_back = lax.all_to_all(grad_slots, 'ep', 1, 0, tiled=True)
        grad_x_moe = jnp.einsum('gsec,egch->gsh', dispatch, grad_back, preferred_element_type=jnp.float32)
        grad_norm_first = jnp.einsum('gsh,gsh->gs', r_loc, out_first, preferred_element_type=jnp.float32).astype(jnp.bfloat16).astype(jnp.float32)
        grad_norm_second = jnp.einsum('gsh,gsh->gs', r_loc, out_second, preferred_element_type=jnp.float32).astype(jnp.bfloat16).astype(jnp.float32)
        gate_sq = gate_sum * gate_sum
        grad_gate_first = (grad_norm_first - grad_norm_second) * gate_second / gate_sq
        grad_gate_second = (grad_norm_second - grad_norm_first) * gate_first / gate_sq
        grad_prob = grad_gate_first[..., None] * first_hot + grad_gate_second[..., None] * second_hot + (ALPHA * hidden * experts) * frac_first
        grad_logits = router_prob * (grad_prob - jnp.sum(router_prob * grad_prob, axis=-1, keepdims=True))
        grad_logits_bf = grad_logits.astype(jnp.bfloat16)
        grad_x_router = jnp.einsum('gse,he->gsh', grad_logits_bf, w_gate, preferred_element_type=jnp.float32)
        grad_x = (r_loc.astype(jnp.float32) + grad_x_moe + grad_x_router).astype(jnp.bfloat16)
        grad_gate_w = lax.psum(jnp.einsum('gsh,gse->he', x_loc, grad_logits_bf, preferred_element_type=jnp.float32), 'ep')
        return loss_value, grad_x, grad_w_in, grad_w_out, grad_gate_w

    row_spec = P('ep', None, None)
    id_spec = P('ep', None)
    return jax.shard_map(layer_body, mesh=mesh, in_specs=(row_spec, row_spec, P(None, None), row_spec, row_spec, id_spec, id_spec, id_spec), out_specs=(P(), row_spec, row_spec, row_spec, P(None, None)), check_vma=False)
```

profile of v0, /device:TPU:0, one launch (start us, length us, event | category | flops | bytes accessed | tf_op | source)
XLA Modules:
  0.0 919.3 jit_solution(6904453473400721069)
XLA Ops:
  7.2 1.3 fusion.65
  8.5 0.9 fusion.73
  9.4 5.0 fusion.81
  14.4 1.6 fusion.93
  16.0 0.2 fusion.71
  16.2 0.8 copy-done.1
  17.0 1.2 fusion.90
  18.2 0.6 fusion.66
  18.8 0.6 fusion.91
  19.4 0.1 fusion.78
  19.5 6.4 fusion.37
  26.0 25.5 %convert_bitcast_fusion.1 = bf16[64,8,16,768]{3,2,0,1:T(8,128)(2,1)} fusion(bf16[8,512,64,16]{1,2,3,0:T(8,128)(2,1)} %get-tuple-element.18, bf16[8,512,768]{2,1,0:T(8,128)(2,1)S(1)} %bitcast.125), kind=kOutput, calls=%fused_computation.55 | convolution fusion | flops 6448742400 | bytes 27262976 | tf_op jit(solution)/shard_map/gsec,gsh->egch/dot_general | solution.py:51
  51.5 10.9 %copy.22 = bf16[64,8,16,768]{3,2,1,0:T(8,128)(2,1)} copy(bf16[64,8,16,768]{3,2,0,1:T(8,128)(2,1)} %convert_bitcast_fusion.1) | data formatting | bytes 25165824 | tf_op jit(solution)/shard_map/convert_element_type | solution.py:51
  62.4 5.5 all-to-all-start
  68.0 15.9 %convert_bitcast_fusion = bf16[64,8,16,768]{3,2,0,1:T(8,128)(2,1)} fusion(bf16[8,512,64,16]{1,2,3,0:T(8,128)(2,1)} %get-tuple-element.17, bf16[8,512,768]{2,1,0:T(8,128)(2,1)} %param.9), kind=kOutput, calls=%fused_computation.54 | convolution fusion | flops 6448742400 | bytes 27262976 | tf_op jit(solution)/shard_map/gsec,gsh->egch/dot_general | solution.py:67
  83.9 11.0 %copy.27 = bf16[64,8,16,768]{3,2,1,0:T(8,128)(2,1)} copy(bf16[64,8,16,768]{3,2,0,1:T(8,128)(2,1)} %convert_bitcast_fusion) | data formatting | bytes 25165824 | tf_op jit(solution)/shard_map/convert_element_type | solution.py:67
  94.9 6.6 fusion.32
  101.5 122.5 %all-to-all-done = bf16[64,8,16,768]{3,2,1,0:T(8,128)(2,1)} async-done(((bf16[64,8,16,768]{3,2,1,0:T(8,128)(2,1)}), bf16[64,8,16,768]{3,2,1,0:T(8,128)(2,1)}, u32[]{:S(2)}, u32[]{:S(2)}) %all-to-all-start) | async-done | bytes 12582944 | tf_op jit(solution)/shard_map/all_to_all | solution.py:52
  224.0 4.4 all-to-all-start.2
  228.4 83.3 %multiply_convert_fusion = (bf16[4,128,16,3072]{3,1,2,0:T(8,128)(2,1)}, f32[4,128,16,3072]{3,1,2,0:T(8,128)}) fusion(bf16[4,768,3072]{2,1,0:T(8,128)(2,1)} %param.11, bf16[16,4,8,16,768]{4,3,2,1,0:T(8,128)(2,1)} %bitcast.9), kind=kOutput, calls=%fused_computation.15 | convolution fusion | flops 38881198080 | bytes 182452224 | tf_op jit(solution)/shard_map/egch,ehf->egcf/dot_general | solution.py:53
  311.7 48.1 %fusion.46 = bf16[4,128,16,768]{3,1,2,0:T(8,128)(2,1)} fusion(bf16[4,128,16,3072]{3,1,2,0:T(8,128)(2,1)} %get-tuple-element.27, bf16[4,3072,768]{2,1,0:T(8,128)(2,1)} %param.12), kind=kOutput, calls=%fused_computation.65 | convolution fusion | flops 38660997120 | bytes 81788928 | tf_op jit(solution)/shard_map/egcf,efh->egch/dot_general | solution.py:55
  359.8 14.1 %copy.24 = bf16[4,128,16,768]{3,2,0,1:T(8,128)(2,1)} copy(bf16[4,128,16,768]{3,1,2,0:T(8,128)(2,1)} %fusion.46) | data formatting | bytes 25165824 | tf_op jit(solution)/shard_map/convert_element_type | solution.py:55
  373.9 10.6 %all-to-all-done.2 = bf16[64,8,16,768]{3,2,1,0:T(8,128)(2,1)} async-done(((bf16[64,8,16,768]{3,2,1,0:T(8,128)(2,1)}), bf16[64,8,16,768]{3,2,1,0:T(8,128)(2,1)}, u32[]{:S(2)}, u32[]{:S(2)}) %all-to-all-start.2) | async-done | bytes 12582944 | tf_op jit(solution)/shard_map/all_to_all | solution.py:68
  384.5 4.3 all-to-all-start.1
  388.8 112.1 %fusion.3 = bf16[4,128,16,3072]{3,1,2,0:T(8,128)(2,1)} fusion(f32[4,128,16,3072]{3,1,2,0:T(8,128)} %get-tuple-element.28, bf16[4,3072,768]{2,1,0:T(8,128)(2,1)} %param.12, bf16[16,4,8,16,768]{4,3,2,1,0:T(8,128)(2,1)} %bitcast.27), kind=kOutput, calls=%fused_computation.7 | convolution fusion | flops 39208353792 | bytes 182452224 | tf_op jit(solution)/shard_map/egch,efh->egcf/dot_general | solution.py:70
  500.9 48.3 %fusion.49 = bf16[4,128,16,768]{3,1,2,0:T(8,128)(2,1)} fusion(bf16[4,128,16,3072]{3,1,2,0:T(8,128)(2,1)} %fusion.3, bf16[4,768,3072]{2,1,0:T(8,128)(2,1)} %param.11), kind=kOutput, calls=%fused_computation.66 | convolution fusion | flops 38660997120 | bytes 81788928 | tf_op jit(solution)/shard_map/egcf,ehf->egch/dot_general | solution.py:73
  549.2 14.3 %copy.29 = bf16[4,128,16,768]{3,2,0,1:T(8,128)(2,1)} copy(bf16[4,128,16,768]{3,1,2,0:T(8,128)(2,1)} %fusion.49) | data formatting | bytes 25165824 | tf_op jit(solution)/shard_map/convert_element_type | solution.py:73
  563.4 84.9 %bitcast_convert_fusion = bf16[4,3072,768]{2,1,0:T(8,128)(2,1)} fusion(bf16[4,128,16,3072]{3,1,2,0:T(8,128)(2,1)} %get-tuple-element.27, bf16[16,4,8,16,768]{4,3,2,1,0:T(8,128)(2,1)} %bitcast.27), kind=kOutput, calls=%fused_computation.16 | convolution fusion | flops 38664142848 | bytes 81788928 | tf_op jit(solution)/shard_map/egcf,egch->efh/dot_general | solution.py:69
  648.4 4.0 all-to-all-start.3
  652.3 0.0 all-reduce.2.cloned.1.call-start
  652.4 50.8 %bitcast_convert_fusion.1 = bf16[4,768,3072]{2,1,0:T(8,128)(2,1)} fusion(bf16[4,128,16,3072]{3,1,2,0:T(8,128)(2,1)} %fusion.3, bf16[16,4,8,16,768]{4,3,2,1,0:T(8,128)(2,1)} %bitcast.9), kind=kOutput, calls=%fused_computation.17 | convolution fusion | flops 38664142848 | bytes 81788928 | tf_op jit(solution)/shard_map/egch,egcf->ehf/dot_general | solution.py:72
  703.2 13.2 %copy.90 = bf16[4,16,8,16,768]{4,0,1,3,2:T(4,128)(2,1)} copy(bf16[4,16,8,16,768]{4,3,0,2,1:T(8,128)(2,1)} %bitcast.16) | data formatting | bytes 25165824 | tf_op jit(solution)/shard_map/all_to_all | solution.py:56
  716.4 20.5 %all_to_all.59 = bf16[64,8,16,768]{3,0,2,1:T(8,128)(2,1)} reshape(bf16[16,4,8,16,768]{4,1,0,3,2:T(4,128)(2,1)} %bitcast.122) | data formatting | bytes 25165824 | tf_op jit(solution)/shard_map/all_to_all | solution.py:56
  736.9 13.6 %bitcast_convert_fusion.2 = bf16[8,512,768]{2,1,0:T(8,128)(2,1)} fusion(bf16[64,8,16,768]{3,0,2,1:T(8,128)(2,1)} %all_to_all.59, bf16[8,512,16]{1,2,0:T(8,128)(2,1)S(1)} %copy-done.13, bf16[8,512,64]{1,2,0:T(8,128)(2,1)S(1)} %copy-done.8), kind=kOutput, calls=%fused_computation.48 | convolution fusion | flops 6449790976 | bytes 19529728 | tf_op jit(solution)/shard_map/gsec,egch->gsh/dot_general | solution.py:58
  750.7 15.7 %fusion.26 = (bf16[8,512]{1,0:T(8,128)(2,1)}, f32[]{:T(128)}, bf16[8,512]{1,0:T(8,128)(2,1)}) fusion(bf16[8,512,768]{2,1,0:T(8,128)(2,1)S(1)} %bitcast.129, bf16[8,512,768]{2,1,0:T(8,128)(2,1)} %bitcast_convert_fusion.2, f32[8,512]{1,0:T(8,128)S(1)} %copy-done.23, f32[8,512]{1,0:T(8,128)S(1)} %copy-done.22, bf16[64,8,16,768]{3,0,2,1:T(8,128)(2,1)} %all_to_all.59, ...), kind=kOutput, calls=%fused_computation.42 | convolution fusion | flops 6487531520 | bytes 25870340 | tf_op jit(solution)/shard_map/gsec,egch->gsh/dot_general | solution.py:57
  767.7 0.8 pad_maximum_fusion
  768.5 66.6 %psum.14 = f32[129]{0:T(256)S(1)} all-reduce(f32[129]{0:T(256)S(1)} %pad_maximum_fusion), channel_id=1, replica_groups=mesh['ep'=16] {'ep'}, use_global_device_ids=true, to_apply=%region_10.0 | all-reduce | flops 129 | bytes 1032 | tf_op jit(solution)/shard_map/psum | solution.py:62
  835.0 0.7 slice_multiply_fusion
  835.8 0.8 fusion.85
  836.6 0.5 multiply_reduce_fusion
  837.1 5.7 convolution_bitcast_fusion.1
  842.8 13.3 %copy.89 = bf16[4,16,8,16,768]{4,0,1,3,2:T(4,128)(2,1)} copy(bf16[4,16,8,16,768]{4,3,0,2,1:T(8,128)(2,1)} %bitcast.32) | data formatting | bytes 25165824 | tf_op jit(solution)/shard_map/all_to_all | solution.py:74
  856.1 20.5 %all_to_all.67 = bf16[64,8,16,768]{3,0,2,1:T(8,128)(2,1)} reshape(bf16[16,4,8,16,768]{4,1,0,3,2:T(4,128)(2,1)} %bitcast.123) | data formatting | bytes 25165824 | tf_op jit(solution)/shard_map/all_to_all | solution.py:74
  876.5 14.5 %fusion.89 = f32[8,512,768,1]{2,1,3,0:T(8,128)} fusion(bf16[64,8,16,768]{3,0,2,1:T(8,128)(2,1)} %all_to_all.67, bf16[8,512,16]{1,2,0:T(8,128)(2,1)S(1)} %copy-done.13, bf16[8,512,64]{1,2,0:T(8,128)(2,1)S(1)} %copy-done.9, bf16[8,512,16]{1,2,0:T(8,128)(2,1)S(1)} %copy-done.11, bf16[8,512,64]{1,2,0:T(8,128)(2,1)S(1)} %copy-done.6), kind=kOutput, calls=%fused_computation.123 | convolution fusion | flops 6455033856 | bytes 26476544 | tf_op jit(solution)/shard_map/gsec,egch->gsh/dot_general | solution.py:75
  891.0 11.7 %fusion.25 = bf16[8,512,768]{2,1,0:T(8,128)(2,1)} fusion(bf16[8,512,768]{2,1,0:T(8,128)(2,1)} %param.9, f32[8,512,768,1]{2,1,3,0:T(8,128)} %fusion.89, bf16[768,64]{0,1:T(8,128)(2,1)S(1)} %copy-done, f32[8,512]{1,0:T(8,128)S(1)} %multiply_reduce_fusion, f32[64]{0:T(128)S(1)} %get-tuple-element.23, f32[8,512]{1,0:T(8,128)S(1)} %get-tuple-element.20, ...), kind=kOutput, calls=%fused_computation.41 | convolution fusion | flops 419172416 | bytes 26411264 | tf_op jit(solution)/shard_map/gse,he->gsh/dot_general | solution.py:84
  902.7 0.5 slice.9
  904.5 4.7 all-reduce.2.cloned.1.call-done
  909.3 1.6 copy.92
  (68 shorter events, 0.2 us)
Async XLA Ops:
  7.2 2.2 copy-start
  7.2 9.8 %copy-start.16 = (s32[8,512]{1,0:T(8,128)S(1)}, s32[8,512]{1,0:T(8,128)}, u32[]{:S(2)}) copy-start(s32[8,512]{1,0:T(8,128)} %param.13) | copy-start | bytes 49156
  7.2 8.8 copy-start.24
  7.2 8.8 copy-start.18
  9.4 16.6 %copy-start.4 = (bf16[8,512,64]{1,2,0:T(8,128)(2,1)}, bf16[8,512,64]{1,2,0:T(8,128)(2,1)S(1)}, u32[]{:S(2)}) copy-start(bf16[8,512,64]{1,2,0:T(8,128)(2,1)S(1)} %fusion.73) | copy-start | bytes 1572868
  14.4 3.8 copy-start.3
  14.4 11.6 %slice-start = ((s8[6291456]{0:T(1024)(128)(4,1)}), s8[4194304]{0:T(1024)(128)(4,1)S(1)}, s32[]{:S(2)}) async-start(s8[6291456]{0:T(1024)(128)(4,1)} %bitcast.124), calls=%async_computation.5 | async-start | bytes 8388608
  16.0 1.0 copy-start.1
  16.0 2.7 copy-start.14
  16.2 3.3 copy-start.7
  18.2 1.2 copy-start.20
  18.2 1.3 copy-start.21
  19.5 6.5 copy-start.10
  19.5 6.5 copy-start.12
  19.5 6.5 slice-start.1
  62.4 32.5 %slice-start.2 = ((s8[6291456]{0:T(1024)(128)(4,1)}), s8[2097152]{0:T(1024)(128)(4,1)S(1)}, s32[]{:S(2)}) async-start(s8[6291456]{0:T(1024)(128)(4,1)} %bitcast.126), calls=%async_computation.7 | async-start | bytes 4194304
  62.4 161.6 %all-to-all-start = ((bf16[64,8,16,768]{3,2,1,0:T(8,128)(2,1)}), bf16[64,8,16,768]{3,2,1,0:T(8,128)(2,1)}, u32[]{:S(2)}, u32[]{:S(2)}) async-start(bf16[64,8,16,768]{3,2,1,0:T(8,128)(2,1)} %copy.22), calls=%async_computation | async-start | bytes 25165824 | tf_op jit(solution)/shard_map/all_to_all | solution.py:52
  68.0 26.9 %slice-start.3 = ((s8[6291456]{0:T(1024)(128)(4,1)}), s8[4194304]{0:T(1024)(128)(4,1)S(1)}, s32[]{:S(2)}) async-start(s8[6291456]{0:T(1024)(128)(4,1)} %bitcast.126), calls=%async_computation.8 | async-start | bytes 8388608
  224.0 160.4 %all-to-all-start.2 = ((bf16[64,8,16,768]{3,2,1,0:T(8,128)(2,1)}), bf16[64,8,16,768]{3,2,1,0:T(8,128)(2,1)}, u32[]{:S(2)}, u32[]{:S(2)}) async-start(bf16[64,8,16,768]{3,2,1,0:T(8,128)(2,1)} %copy.27), calls=%async_computation.2 | async-start | bytes 25165824 | tf_op jit(solution)/shard_map/all_to_all | solution.py:68
  384.5 263.9 %all-to-all-start.1 = ((bf16[4,128,16,768]{3,2,0,1:T(8,128)(2,1)}), bf16[4,128,16,768]{3,2,0,1:T(8,128)(2,1)}, u32[]{:S(2)}, u32[]{:S(2)}) async-start(bf16[4,128,16,768]{3,2,0,1:T(8,128)(2,1)} %copy.24), calls=%async_computation.1 | async-start | bytes 25165824 | tf_op jit(solution)/shard_map/all_to_all | solution.py:56
  648.4 194.4 %all-to-all-start.3 = ((bf16[4,128,16,768]{3,2,0,1:T(8,128)(2,1)}), bf16[4,128,16,768]{3,2,0,1:T(8,128)(2,1)}, u32[]{:S(2)}, u32[]{:S(2)}) async-start(bf16[4,128,16,768]{3,2,0,1:T(8,128)(2,1)} %copy.29), calls=%async_computation.3 | async-start | bytes 25165824 | tf_op jit(solution)/shard_map/all_to_all | solution.py:74
  652.3 257.0 %all-reduce.2.cloned.1.call-start = ((), (), s32[]{:S(2)}) async-start(), calls=%async_computation.4 | async-start | bytes 393216 | tf_op jit(solution)/shard_map/psum | solution.py:86
  716.4 20.5 %copy-start.8 = (bf16[8,512,64]{1,2,0:T(8,128)(2,1)S(1)}, bf16[8,512,64]{1,2,0:T(8,128)(2,1)}, u32[]{:S(2)}) copy-start(bf16[8,512,64]{1,2,0:T(8,128)(2,1)} %copy-done.7) | copy-start | bytes 1572868
  716.4 20.5 %copy-start.13 = (bf16[8,512,16]{1,2,0:T(8,128)(2,1)S(1)}, bf16[8,512,16]{1,2,0:T(8,128)(2,1)}, u32[]{:S(2)}) copy-start(bf16[8,512,16]{1,2,0:T(8,128)(2,1)} %copy-done.12) | copy-start | bytes 393220
  716.4 34.2 %slice-start.4 = ((s8[6291456]{0:T(1024)(128)(4,1)}), s8[2097152]{0:T(1024)(128)(4,1)S(1)}, s32[]{:S(2)}) async-start(s8[6291456]{0:T(1024)(128)(4,1)} %bitcast.128), calls=%async_computation.9 | async-start | bytes 4194304
  736.9 13.7 %slice-start.5 = ((s8[6291456]{0:T(1024)(128)(4,1)}), s8[4194304]{0:T(1024)(128)(4,1)S(1)}, s32[]{:S(2)}) async-start(s8[6291456]{0:T(1024)(128)(4,1)} %bitcast.128), calls=%async_computation.10 | async-start | bytes 8388608
  736.9 13.7 %copy-start.5 = (bf16[8,512,64]{1,2,0:T(8,128)(2,1)S(1)}, bf16[8,512,64]{1,2,0:T(8,128)(2,1)}, u32[]{:S(2)}) copy-start(bf16[8,512,64]{1,2,0:T(8,128)(2,1)} %copy-done.4) | copy-start | bytes 1572868
  736.9 13.7 %copy-start.11 = (bf16[8,512,16]{1,2,0:T(8,128)(2,1)S(1)}, bf16[8,512,16]{1,2,0:T(8,128)(2,1)}, u32[]{:S(2)}) copy-start(bf16[8,512,16]{1,2,0:T(8,128)(2,1)} %copy-done.10) | copy-start | bytes 393220
  736.9 13.7 %copy-start.22 = (f32[8,512]{1,0:T(8,128)S(1)}, f32[8,512]{1,0:T(8,128)}, u32[]{:S(2)}) copy-start(f32[8,512]{1,0:T(8,128)} %get-tuple-element.13) | copy-start | bytes 49156
  736.9 13.7 %copy-start.23 = (f32[8,512]{1,0:T(8,128)S(1)}, f32[8,512]{1,0:T(8,128)}, u32[]{:S(2)}) copy-start(f32[8,512]{1,0:T(8,128)} %get-tuple-element.21) | copy-start | bytes 49156
  750.6 85.9 %copy-start.2 = (f32[8,512,64]{1,2,0:T(8,128)S(1)}, f32[8,512,64]{1,2,0:T(8,128)}, u32[]{:S(2)}) copy-start(f32[8,512,64]{1,2,0:T(8,128)} %copy-done.1) | copy-start | bytes 3145732
  750.6 85.9 %copy-start.15 = (f32[8,512]{1,0:T(8,128)S(1)}, f32[8,512]{1,0:T(8,128)}, u32[]{:S(2)}) copy-start(f32[8,512]{1,0:T(8,128)} %copy-done.14) | copy-start | bytes 49156
  750.6 85.9 %copy-start.17 = (s32[8,512]{1,0:T(8,128)S(1)}, s32[8,512]{1,0:T(8,128)}, u32[]{:S(2)}) copy-start(s32[8,512]{1,0:T(8,128)} %param.13) | copy-start | bytes 49156
  750.7 85.9 %copy-start.19 = (s32[8,512]{1,0:T(8,128)S(1)}, s32[8,512]{1,0:T(8,128)}, u32[]{:S(2)}) copy-start(s32[8,512]{1,0:T(8,128)} %param.14) | copy-start | bytes 49156
  856.1 20.5 %copy-start.6 = (bf16[8,512,64]{1,2,0:T(8,128)(2,1)S(1)}, bf16[8,512,64]{1,2,0:T(8,128)(2,1)}, u32[]{:S(2)}) copy-start(bf16[8,512,64]{1,2,0:T(8,128)(2,1)} %copy-done.4) | copy-start | bytes 1572868
  856.1 20.5 %copy-start.9 = (bf16[8,512,64]{1,2,0:T(8,128)(2,1)S(1)}, bf16[8,512,64]{1,2,0:T(8,128)(2,1)}, u32[]{:S(2)}) copy-start(bf16[8,512,64]{1,2,0:T(8,128)(2,1)} %copy-done.7) | copy-start | bytes 1572868
Sparse Core Ops, SparseCore 0:
  842.9 66.3 all-reduce.1
where the time goes:
time: 929 us; the launch traced here: 919 us
  matrix products  537 us (58%)
  waiting for transfers between devices  138 us (15%)
  local copies, waits for them, and re-layouts  121 us (13%)
  blocking collectives  66.6 us (7%)
  other arithmetic  20.3 us (2%)
  between operations  18.7 us (2%)
  starting transfers between devices  18.2 us (2%)
    all_to_all x1, waiting for transfers between devices, layer_body(): expert_x = lax.all_to_all(send_x, 'ep', 0, 1, tiled=True)  123 us
    dot_general x1, matrix products, layer_body(): jnp.einsum('egch,efh->egcf', grad_y, w_out_loc, preferred_element_type=jn...  112 us
    dot_general x1, matrix products, layer_body(): jnp.einsum('egcf,egch->efh', act_bf, grad_y, preferred_element_type=jnp.f...  84.9 us
    dot_general x1, matrix products, layer_body(): jnp.einsum('egch,ehf->egcf', expert_x, w_in_loc, preferred_element_type=j...  83.3 us
    psum x1, blocking collectives, layer_body(): global_stats = lax.psum(local_stats, 'ep')  66.6 us
    dot_general x1, matrix products, layer_body(): jnp.einsum('egch,egcf->ehf', expert_x, grad_pre, preferred_element_type=j...  50.8 us
    dot_general x1, matrix products, layer_body(): jnp.einsum('egcf,ehf->egch', grad_pre, w_in_loc, preferred_element_type=j...  48.3 us
    dot_general x1, matrix products, layer_body(): jnp.einsum('egcf,efh->egch', act_bf, w_out_loc, preferred_element_type=jn...  48.1 us
  transfers between devices with their start and end apart: 5, of which 3 were waited for; matrix products, arithmetic and copies ran while one was open for 63% of the time, Pallas kernels for 0%

commit v1 on v0

v1 whole, which is shorter than its diff:
```python
import functools

import jax
import jax.numpy as jnp
from jax import lax
from jax.experimental import pallas as pl
from jax.experimental.pallas import tpu as pltpu
from jax.sharding import PartitionSpec as P

ALPHA = 0.01
SOURCES = 4
ORDER = (14, 15, 1, 6, 7, 8, 9, 10, 11, 4, 5, 12, 13, 2, 3)
FF_TILE = 768
VMEM_LIMIT = 64 * 1024 * 1024 - 128 * 1024
GELU_K = 0.7978845608028654
GELU_C = 0.044715

BF16 = jnp.bfloat16
F32 = jnp.float32


def dot(a, b, contract=((1,), (0,))):
    return lax.dot_general(a, b, (contract, ((), ())), preferred_element_type=F32)


def route(first_ids, second_ids, keep_ids, experts, cap_rows):
    seq_len = first_ids.shape[1]
    expert_ids = jnp.arange(experts, dtype=jnp.int32)
    first_hot = (first_ids[..., None] == expert_ids).astype(BF16)
    second_hot = (second_ids[..., None] == expert_ids).astype(BF16)
    second_kept = second_hot * keep_ids.astype(BF16)[..., None]
    seq_ids = jnp.arange(seq_len, dtype=jnp.int32)
    earlier = (seq_ids[:, None] > seq_ids[None, :]).astype(BF16)
    before_first = jnp.einsum('st,gte->gse', earlier, first_hot, preferred_element_type=F32)
    before_second = jnp.einsum('st,gte->gse', earlier, second_kept, preferred_element_type=F32)
    first_count = jnp.sum(first_hot, axis=1, dtype=F32)
    pos_first = jnp.sum(before_first * first_hot, axis=-1).astype(jnp.int32)
    pos_second = jnp.sum((before_second + first_count[:, None, :]) * second_hot, axis=-1).astype(jnp.int32)
    slot_first = jnp.where(pos_first < cap_rows, pos_first, -1)
    slot_second = jnp.where((keep_ids == 1) & (pos_second < cap_rows), pos_second, -1)
    return first_hot, second_hot, first_count, slot_first, slot_second


def dispatch_body(l1_ref, l2_ref, x_ref, r_ref, out_ref):
    local, devices, _, _, cap_rows, hidden = out_ref.shape
    slots, seq_len = devices * cap_rows, x_ref.shape[1]
    ids = lax.broadcasted_iota(jnp.int32, (slots, seq_len), 0)
    for j in range(local):
        hit = (l1_ref[0] - j * slots == ids) | (l2_ref[0] - j * slots == ids)
        hot = jnp.where(hit, 1.0, 0.0).astype(BF16)
        for k, ref in enumerate((x_ref, r_ref)):
            out_ref[j, :, k, 0] = dot(hot, ref[0]).astype(BF16).reshape(devices, cap_rows, hidden)


def dispatch(local, devices, cap_rows, l1, l2, x, r):
    groups, seq_len, hidden = x.shape
    slots = local * devices * cap_rows
    id_spec = pl.BlockSpec((1, 1, seq_len), lambda g: (g, 0, 0))
    row_spec = pl.BlockSpec((1, seq_len, hidden), lambda g: (g, 0, 0))
    return pl.pallas_call(
        dispatch_body,
        out_shape=jax.ShapeDtypeStruct((local, devices, 2, groups, cap_rows, hidden), BF16),
        grid=(groups,),
        in_specs=[id_spec, id_spec, row_spec, row_spec],
        out_specs=pl.BlockSpec((local, devices, 2, 1, cap_rows, hidden), lambda g: (0, 0, 0, g, 0, 0)),
        compiler_params=pltpu.CompilerParams(dimension_semantics=('arbitrary',), vmem_limit_bytes=VMEM_LIMIT),
        cost_estimate=pl.CostEstimate(flops=4 * groups * slots * seq_len * hidden, bytes_accessed=4 * x.size + 4 * groups * slots * hidden, transcendentals=0),
        name='dispatch',
    )(l1[:, None, :], l2[:, None, :], x, r)


def moe_body(ff_tile, send_ref, nstat_ref, w1_ref, w2_ref, recv_ref, dxs_ref, back_ref, dw1_ref, dw2_ref, dsend_ref, dback_ref, stat_ref,
             w1_buf, w2_buf, acc1, acc2, tile, dx_tile, nrecv, dwin,
             in_send, in_recv, out_send, out_recv, n_send, n_recv, d_send, d_recv, w_sem, x_sem, dx_sem, dw_sem, own_sem):
    local, devices, both, hidden = send_ref.shape
    window = both // 2
    ff = w1_ref.shape[2]
    rows = SOURCES * window
    tiles = devices // SOURCES
    me = lax.axis_index('ep')

    core, chip = lax.rem(me, 2), me // 2
    bits = [lax.rem(chip // b, 2) for b in (1, 2, 4)]

    def peer_of(k):
        out = me + (1 - 2 * core) * (k % 2)
        for n, bit in enumerate(bits):
            out = out + 2 ** (n + 1) * (1 - 2 * bit) * (k // 2 ** (n + 1) % 2)
        return out

    def remote(src, dst, s, r, peer):
        return pltpu.make_async_remote_copy(src_ref=src, dst_ref=dst, send_sem=s, recv_sem=r, device_id=(peer,), device_id_type=pl.DeviceIdType.MESH)

    def in_copy(j, k, peer):
        return remote(send_ref.at[j, peer], recv_ref.at[j, me], in_send.at[j, k], in_recv.at[j, k], peer)

    def in_landing(j, k, peer):
        return remote(send_ref.at[j, peer], recv_ref.at[j, peer], in_send.at[j, k], in_recv.at[j, k], peer)

    def out_copy(j, k, peer):
        return remote(dxs_ref.at[j, peer], back_ref.at[j, me], out_send.at[j, k], out_recv.at[j, k], peer)

    def out_landing(j, k, peer):
        return remote(dxs_ref.at[j, peer], back_ref.at[j, peer], out_send.at[j, k], out_recv.at[j, k], peer)

    def n_copy(k, peer):
        return remote(nstat_ref.at[peer], nrecv.at[me], n_send.at[k], n_recv.at[k], peer)

    def n_landing(k, peer):
        return remote(nstat_ref.at[peer], nrecv.at[peer], n_send.at[k], n_recv.at[k], peer)

    def d_copy(k, peer):
        return remote(dsend_ref.at[peer], dback_ref.at[me], d_send.at[k], d_recv.at[k], peer)

    def d_landing(k, peer):
        return remote(dsend_ref.at[peer], dback_ref.at[peer], d_send.at[k], d_recv.at[k], peer)

    def each_peer(fn):
        for k in ORDER:
            fn(k, peer_of(k))

    def start_in(j):
        each_peer(lambda k, peer: in_copy(j, k, peer).start())

    def members(t):
        on = [jnp.where(t == 3 - n, 1, 0) for n in range(3)]
        near = chip + sum(2 ** n * (1 - 2 * bits[n]) * on[n] for n in range(3))
        key = sum(2 ** n * on[n] for n in range(3))
        out = []
        for c, q in ((7 - near, 7 - key), (near, key)):
            out += [(2 * q, 2 * c + core), (2 * q + 1, 2 * c + 1 - core)]
        return out

    def weight_copies(j, slot):
        return (pltpu.make_async_copy(w1_ref.at[j], w1_buf.at[slot], w_sem.at[slot, 0]),
                pltpu.make_async_copy(w2_ref.at[j], w2_buf.at[slot], w_sem.at[slot, 1]))

    def tile_copy(j, s, p, ref):
        return pltpu.make_async_copy(ref.at[j, s], tile.at[p], x_sem.at[p])

    def grad_copies(j, slot):
        return (pltpu.make_async_copy(w1_buf.at[slot], dw1_ref.at[j], dw_sem.at[slot, 0]),
                pltpu.make_async_copy(w2_buf.at[slot], dw2_ref.at[j], dw_sem.at[slot, 1]))

    each_peer(lambda k, peer: n_copy(k, peer).start())
    own = pltpu.make_async_copy(nstat_ref.at[me], nrecv.at[me], own_sem)
    own.start()
    for j in range(local):
        start_in(j)
    for copy in weight_copies(0, 0):
        copy.start()
    own.wait()
    each_peer(lambda k, peer: n_landing(k, peer).wait())
    stat_ref[...] = jnp.sum(nrecv[...], axis=0)
    diag = lax.broadcasted_iota(jnp.int32, (window, window), 0) == lax.broadcasted_iota(jnp.int32, (window, window), 1)

    @pl.loop(0, local * tiles)
    def _(i):
        j = i // tiles
        t = lax.rem(i, tiles)
        wslot = lax.rem(j, 2)
        slot = lax.rem(i, 2)
        sources = members(t)

        @pl.when(t == 0)
        def _():
            for copy in weight_copies(j, wslot):
                copy.wait()
            acc1[...] = jnp.zeros_like(acc1)
            acc2[...] = jnp.zeros_like(acc2)

        @pl.when((t == 1) & (j > 0))
        def _():
            for copy in grad_copies(j - 1, 1 - wslot):
                copy.wait()

        @pl.when((t == 1) & (j + 1 < local))
        def _():
            for copy in weight_copies(j + 1, 1 - wslot):
                copy.start()

        for p, (k, s) in enumerate(sources):
            if p == 2:
                @pl.when(t == 0)
                def _():
                    tile_copy(j, s, p, send_ref).start()

                @pl.when(t > 0)
                def _():
                    in_landing(j, k, s).wait_recv()
                    tile_copy(j, s, p, recv_ref).start()
            else:
                in_landing(j, k, s).wait_recv()
                tile_copy(j, s, p, recv_ref).start()
        for p, (k, s) in enumerate(sources):
            tile_copy(j, s, p, recv_ref).wait()

        x = tile[:, :window].reshape(rows, hidden)
        r = tile[:, window:].reshape(rows, hidden).astype(F32)
        weights = [jnp.sum(jnp.where(diag, nrecv[s, pl.ds(j, 1), :], 0.0), axis=1, keepdims=True) for _, s in sources]
        g = (r * jnp.concatenate(weights, axis=0)).astype(BF16)
        h = None
        dx = None
        for f0 in range(0, ff, ff_tile):
            w1 = w1_buf[wslot, :, f0:f0 + ff_tile]
            w2 = w2_buf[wslot, f0:f0 + ff_tile, :]
            pre = dot(x, w1)
            sq = pre * pre
            th = jnp.tanh(pre * (GELU_K + (GELU_K * GELU_C) * sq))
            half = 0.5 + 0.5 * th
            act = (pre * half).astype(BF16)
            slope = half + (0.5 * pre) * (1.0 - th * th) * (GELU_K + (3.0 * GELU_K * GELU_C) * sq)
            ga = dot(g, w2, ((1,), (1,))).astype(BF16).astype(F32)
            gp = (ga * slope).astype(BF16)
            hp = dot(act, w2)
            h = hp if h is None else h + hp
            dp = dot(gp, w1, ((1,), (1,)))
            dx = dp if dx is None else dx + dp
            acc1[:, f0:f0 + ff_tile] += dot(x, gp, ((0,), (0,)))
            acc2[f0:f0 + ff_tile, :] += dot(act, g, ((0,), (0,)))
        dx_tile[slot] = dx.astype(BF16).reshape(SOURCES, window, hidden)
        stores = [pltpu.make_async_copy(dx_tile.at[slot, p], dxs_ref.at[j, s], dx_sem.at[p]) for p, (_, s) in enumerate(sources)]
        for p, copy in enumerate(stores):
            if p != 2:
                copy.start()

        @pl.when(t > 0)
        def _():
            stores[2].start()

        @pl.when(t == 0)
        def _():
            kept = pltpu.make_async_copy(dx_tile.at[slot, 2], back_ref.at[j, me], dx_sem.at[2])
            kept.start()

        d = jnp.sum(r * h.astype(BF16).astype(F32), axis=1, keepdims=True)
        for p, (_, s) in enumerate(sources):
            dwin[s, pl.ds(j, 1), :] = jnp.sum(jnp.where(diag, d[p * window:(p + 1) * window], 0.0), axis=0, keepdims=True)
        for p, (k, s) in enumerate(sources):
            stores[p].wait()
            if p == 2:
                @pl.when(t > 0)
                def _():
                    out_copy(j, k, s).start()
            else:
                out_copy(j, k, s).start()

        @pl.when(t == tiles - 1)
        def _():
            w1_buf[wslot] = acc1[...].astype(BF16)
            w2_buf[wslot] = acc2[...].astype(BF16)
            for copy in grad_copies(j, wslot):
                copy.start()

    saved = pltpu.make_async_copy(dwin, dsend_ref, own_sem)
    saved.start()
    saved.wait()
    each_peer(lambda k, peer: d_copy(k, peer).start())
    own = pltpu.make_async_copy(dwin.at[me], dback_ref.at[me], own_sem)
    own.start()
    own.wait()
    for copy in grad_copies(local - 1, (local - 1) % 2):
        copy.wait()
    each_peer(lambda k, peer: d_landing(k, peer).wait())

    @pl.loop(0, local)
    def _(j):
        each_peer(lambda k, peer: in_copy(j, k, peer).wait_send())
        each_peer(lambda k, peer: out_landing(j, k, peer).wait())


def moe(send, nstat, w_in, w_out):
    local, devices, both, hidden = send.shape
    window = both // 2
    ff = w_in.shape[2]
    anywhere = pl.BlockSpec(memory_space=pl.ANY)
    slots = jax.ShapeDtypeStruct((local, devices, window, hidden), BF16)
    small = jax.ShapeDtypeStruct(nstat.shape, F32)
    dma = pltpu.SemaphoreType.DMA
    return pl.pallas_call(
        functools.partial(moe_body, FF_TILE),
        out_shape=(
            jax.ShapeDtypeStruct(send.shape, BF16), slots, slots,
            jax.ShapeDtypeStruct(w_in.shape, BF16), jax.ShapeDtypeStruct(w_out.shape, BF16),
            small, small, jax.ShapeDtypeStruct(nstat.shape[1:], F32),
        ),
        in_specs=[anywhere] * 4,
        out_specs=(anywhere,) * 7 + (pl.BlockSpec(memory_space=pltpu.VMEM),),
        scratch_shapes=[
            pltpu.VMEM((2, hidden, ff), BF16), pltpu.VMEM((2, ff, hidden), BF16),
            pltpu.VMEM((hidden, ff), F32), pltpu.VMEM((ff, hidden), F32),
            pltpu.VMEM((SOURCES, both, hidden), BF16), pltpu.VMEM((2, SOURCES, window, hidden), BF16),
            pltpu.VMEM(nstat.shape, F32), pltpu.VMEM(nstat.shape, F32),
            dma((local, devices)), dma((local, devices)), dma((local, devices)), dma((local, devices)),
            dma((devices,)), dma((devices,)), dma((devices,)), dma((devices,)),
            dma((2, 2)), dma((SOURCES,)), dma((SOURCES,)), dma((2, 2)), dma,
        ],
        compiler_params=pltpu.CompilerParams(has_side_effects=True, vmem_limit_bytes=VMEM_LIMIT),
        cost_estimate=pl.CostEstimate(flops=12 * local * devices * window * hidden * ff, bytes_accessed=8 * local * hidden * ff, transcendentals=local * devices * window * ff),
        name='moe',
    )(send, nstat, w_in, w_out)


def combine_body(l1_ref, l2_ref, back_ref, res_ref, gl_ref, wg_ref, out_ref):
    local, devices, _, cap_rows, hidden = back_ref.shape
    seq_len = l1_ref.shape[2]
    slots = local * devices * cap_rows
    ids = lax.broadcasted_iota(jnp.int32, (slots, seq_len), 0)
    hit = (l1_ref[0] == ids) | (l2_ref[0] == ids)
    hot = jnp.where(hit, 1.0, 0.0).astype(BF16)
    total = dot(hot, back_ref[...].reshape(slots, hidden), ((0,), (0,)))
    total += res_ref[0].astype(F32)
    total += dot(gl_ref[0], wg_ref[...], ((1,), (1,)))
    out_ref[0] = total.astype(out_ref.dtype)


def combine(l1, l2, back, res, grad_logits, w_gate):
    groups, seq_len, hidden = res.shape
    local, devices, _, cap_rows, _ = back.shape
    slots = local * devices * cap_rows
    experts = w_gate.shape[1]
    id_spec = pl.BlockSpec((1, 1, seq_len), lambda g: (g, 0, 0))
    row_spec = pl.BlockSpec((1, seq_len, hidden), lambda g: (g, 0, 0))
    return pl.pallas_call(
        combine_body,
        out_shape=jax.ShapeDtypeStruct(res.shape, BF16),
        grid=(groups,),
        in_specs=[
            id_spec, id_spec, pl.BlockSpec((local, devices, 1, cap_rows, hidden), lambda g: (0, 0, g, 0, 0)), row_spec,
            pl.BlockSpec((1, seq_len, experts), lambda g: (g, 0, 0)), pl.BlockSpec((hidden, experts), lambda g: (0, 0)),
        ],
        out_specs=row_spec,
        compiler_params=pltpu.CompilerParams(dimension_semantics=('arbitrary',), vmem_limit_bytes=VMEM_LIMIT),
        cost_estimate=pl.CostEstimate(flops=2 * groups * slots * seq_len * hidden, bytes_accessed=2 * groups * slots * hidden + 6 * res.size, transcendentals=0),
        name='combine',
    )(l1[:, None, :], l2[:, None, :], back, res, grad_logits, w_gate)


def solution(mesh):
    ep_size = mesh.shape['ep']

    def layer_body(x_loc, r_loc, w_gate, w_in_loc, w_out_loc, first_ids, second_ids, keep_ids):
        local_groups, seq_len, hidden = x_loc.shape
        experts = w_gate.shape[1]
        local = experts // ep_size
        cap_rows = 2 * seq_len // experts
        region = local_groups * cap_rows
        tokens_all = local_groups * ep_size * seq_len
        numel = tokens_all * hidden

        first_hot, second_hot, first_count, slot_first, slot_second = route(first_ids, second_ids, keep_ids, experts, cap_rows)

        def slot_of(slot, expert_of):
            return jnp.where(slot >= 0, ((expert_of % local) * ep_size + expert_of // local) * cap_rows + slot, -1)

        l1, l2 = slot_of(slot_first, first_ids), slot_of(slot_second, second_ids)
        send = dispatch(local, ep_size, cap_rows, l1, l2, x_loc, r_loc).reshape(local, ep_size, 2 * region, hidden)

        logits = jnp.einsum('gsh,he->gse', x_loc, w_gate, preferred_element_type=F32)
        router_prob = jax.nn.softmax(logits, axis=-1)
        gate_first = jnp.sum(router_prob * first_hot, axis=-1)
        gate_second = jnp.sum(router_prob * second_hot, axis=-1)
        gate_sum = gate_first + gate_second
        norm_first = (gate_first / gate_sum).astype(BF16)
        norm_second = (gate_second / gate_sum).astype(BF16)
        slot_ids = jnp.arange(cap_rows, dtype=jnp.int32)
        slot_hot_first = (slot_first[..., None] == slot_ids).astype(BF16)
        slot_hot_second = (slot_second[..., None] == slot_ids).astype(BF16)
        nwin = (jnp.einsum('gse,gsc->egc', first_hot, slot_hot_first * norm_first[..., None], preferred_element_type=F32)
                + jnp.einsum('gse,gsc->egc', second_hot, slot_hot_second * norm_second[..., None], preferred_element_type=F32))
        stats = jnp.concatenate([jnp.sum(first_count, axis=0), jnp.sum(router_prob, axis=(0, 1))])
        nwin_rows = nwin.reshape(ep_size, local, region)
        stat_rows = jnp.broadcast_to(jnp.pad(stats, (0, region - 2 * experts)), (ep_size, 1, region))
        nstat = jnp.concatenate([nwin_rows, stat_rows, jnp.zeros((ep_size, 7 - local, region), F32)], axis=1)
        _, _, back, dw1, dw2, _, dback, stats = moe(send, nstat, w_in_loc, w_out_loc)
        frac_first = stats[local, :experts] / tokens_all
        mean_prob = stats[local, experts:2 * experts] / tokens_all
        dwin = dback[:, :local].reshape(experts, local_groups, cap_rows)
        dot_sum = jnp.einsum('gsh,gsh->', x_loc, r_loc, preferred_element_type=F32) + jnp.sum(nwin * dwin)
        dwin_bf = dwin.astype(BF16)
        d_first = jnp.einsum('gse,egc->gsc', first_hot, dwin_bf, preferred_element_type=F32)
        d_second = jnp.einsum('gse,egc->gsc', second_hot, dwin_bf, preferred_element_type=F32)
        grad_norm_first = jnp.sum(d_first * slot_hot_first, axis=-1)
        grad_norm_second = jnp.sum(d_second * slot_hot_second, axis=-1)
        gate_sq = gate_sum * gate_sum
        grad_gate_first = (grad_norm_first - grad_norm_second) * gate_second / gate_sq
        grad_gate_second = (grad_norm_second - grad_norm_first) * gate_first / gate_sq
        grad_prob = grad_gate_first[..., None] * first_hot + grad_gate_second[..., None] * second_hot + (ALPHA * hidden * experts) * frac_first
        grad_logits = router_prob * (grad_prob - jnp.sum(router_prob * grad_prob, axis=-1, keepdims=True))
        grad_logits_bf = grad_logits.astype(BF16)
        grad_gate_local = jnp.einsum('gsh,gse->he', x_loc, grad_logits_bf, preferred_element_type=F32)
        grad_gate_w, dot_all = lax.psum((grad_gate_local, dot_sum[None]), 'ep')
        loss_value = dot_all[0] / numel + ALPHA * experts * jnp.sum(frac_first * mean_prob)

        grad_x = combine(l1, l2, back.reshape(local, ep_size, local_groups, cap_rows, hidden), r_loc, grad_logits_bf, w_gate)
        return loss_value, grad_x, dw1, dw2, grad_gate_w

    row_spec = P('ep', None, None)
    id_spec = P('ep', None)
    return jax.shard_map(layer_body, mesh=mesh, in_specs=(row_spec, row_spec, P(None, None), row_spec, row_spec, id_spec, id_spec, id_spec), out_specs=(P(), row_spec, row_spec, row_spec, P(None, None)), check_vma=False)
```

time: 929 us -> 597 us (0.64)
  matrix products: 537 us -> 16.5 us
  Pallas kernels: 0 us -> 457 us
  waiting for transfers between devices: 138 us -> 3.46 us
  local copies, waits for them, and re-layouts: 121 us -> 39.8 us
  blocking collectives: 66.6 us -> 32.3 us
  starting transfers between devices: 18.2 us -> 0.04 us
    dot_general x16 -> x8, matrix products: 537 us -> 16.5 us  [the longest x1 4.8 us: layer_body(): jnp.einsum('gsh,he->gse', x_loc, w_gate, preferred_element_type=F32)]
    pallas_call x0 -> x3, Pallas kernels: none -> 457 us  [the longest x1 422 us: moe(): pl.pallas_call(functools.partial(moe_body, FF_TILE), out_shape=(jax.Shape...]
    all_to_all x4 -> x0, waiting for transfers between devices: 133 us -> none  [the longest x1 123 us: layer_body(): expert_x = lax.all_to_all(send_x, 'ep', 0, 1, tiled=True)]
    all_to_all x4 -> x0, local copies, waits for them, and re-layouts: 67.4 us -> none  [the longest x2 33.7 us: layer_body(): grad_back = lax.all_to_all(grad_slots, 'ep', 1, 0, tiled=True)]
    convert_element_type x4 -> x0, local copies, waits for them, and re-layouts: 50.2 us -> none  [the longest x1 14.3 us: layer_body(): jnp.einsum('egcf,ehf->egch', grad_pre, w_in_loc, preferred_element_type=j...]
    psum x1, blocking collectives: 66.6 us -> 32.3 us  [layer_body(): grad_gate_w, dot_all = lax.psum((grad_gate_local, dot_sum[None]), 'ep')]
    unnamed x63 -> x56, local copies, waits for them, and re-layouts: 2.54 us -> 36.4 us
    all_to_all x4 -> x0, starting transfers between devices: 18.1 us -> none  [the longest x1 5.52 us: layer_body(): expert_x = lax.all_to_all(send_x, 'ep', 0, 1, tiled=True)]
  transfers between devices with their start and end apart: 5 -> 1, of which waited for: 3 -> 1; matrix products, arithmetic and copies ran while one was open for 63% -> 2% of each run, Pallas kernels for 0% -> 3%
where the time goes in v1:
time: 597 us; the launch traced here: 595 us
  Pallas kernels  457 us (77%)
  local copies, waits for them, and re-layouts  39.8 us (7%)
  blocking collectives  32.3 us (5%)
  other arithmetic  27.4 us (5%)
  between operations  18.1 us (3%)
  matrix products  16.5 us (3%)
    pallas_call x1, Pallas kernels, moe(): pl.pallas_call(functools.partial(moe_body, FF_TILE), out_shape=(jax.Shape...  422 us
    unnamed x56, local copies, waits for them, and re-layouts  36.4 us
    psum x1, blocking collectives, layer_body(): grad_gate_w, dot_all = lax.psum((grad_gate_local, dot_sum[None]), 'ep')  32.3 us
    pallas_call x1, Pallas kernels, dispatch(): pl.pallas_call(dispatch_body, out_shape=jax.ShapeDtypeStruct((local, devi...  20 us
    pallas_call x1, Pallas kernels, combine(): pl.pallas_call(combine_body, out_shape=jax.ShapeDtypeStruct(res.shape, BF...  15.5 us
  transfers between devices with their start and end apart: 1, of which 1 were waited for; matrix products, arithmetic and copies ran while one was open for 2% of the time, Pallas kernels for 3%

profile of v1, /device:TPU:0, one launch (start us, length us, event | category | flops | bytes accessed | tf_op | source)
XLA Modules:
  0.0 595.1 jit_solution(17772859121354760615)
XLA Ops:
  7.2 0.0 all-reduce.2.cloned.1.call-start
  7.2 4.8 fusion.74
  12.0 0.0 copy-start.21
  12.0 0.0 copy-start.11
  12.1 0.6 copy.31
  12.7 0.1 copy-done.21
  12.8 0.0 copy-done.11
  12.8 2.5 fusion.5
  15.3 1.3 fusion.15
  16.7 4.2 fusion.73
  20.9 0.0 copy-start.17
  20.9 3.0 fusion.2
  24.0 0.0 copy-start.24
  24.0 1.3 fusion.8
  25.4 1.3 fusion.21
  26.7 0.2 copy.37
  26.8 0.1 reshape.86
  27.0 0.3 copy-done.13
  27.3 0.6 broadcast_in_dim.19.l2_ref
  27.9 0.6 copy.36.l1_ref
  28.5 0.1 pad_maximum_fusion
  28.6 0.1 pad.2.clone
  28.7 0.7 maximum_maximum_fusion.nstat_ref
  29.4 20.0 %dispatch.1 = bf16[4,16,2,8,16,768]{5,4,3,2,1,0:T(8,128)(2,1)} custom-call(s32[8,1,512]{2,1,0:T(1,128)} %copy.36.l1_ref, s32[8,1,512]{2,1,0:T(1,128)} %broadcast_in_dim.19.l2_ref, bf16[8,512,768]{2,1,0:T(8,128)(2,1)} %x_ref.1, bf16[8,512,768]{2,1,0:T(8,128)(2,1)} %res_ref.1), custom_call_target="tpu_custom_call" | custom-call | flops 12884901888 | bytes 37748736 | tf_op jit(solution)/shard_map/dispatch/pallas_call | solution.py:60
  49.5 0.0 copy-start.25
  49.5 421.9 %moe.1 = (bf16[4,16,256,768]{3,2,1,0:T(8,128)(2,1)}, bf16[4,16,128,768]{3,2,1,0:T(8,128)(2,1)}, bf16[4,16,128,768]{3,2,1,0:T(8,128)(2,1)}, bf16[4,768,3072]{2,1,...) custom-call(bf16[4,16,256,768]{3,2,1,0:T(8,128)(2,1)} %bitcast.35, ...), custom_call_target="tpu_custom_call" | custom-call | flops 231928233984 | bytes 75497472 | tf_op jit(solution)/shard_map/moe/pallas_call | solution.py:280
  471.4 0.0 copy-start.2
  471.4 1.0 slice.9
  472.4 0.1 reshape.87
  472.6 0.1 copy.38
  472.7 1.0 fusion.18
  473.7 1.0 fusion.19
  474.7 1.9 multiply_bitcast_fusion
  476.6 4.7 multiply_reduce_fusion
  481.3 4.5 multiply_convert_fusion.gl_ref
  485.9 0.0 copy-start.3
  485.9 1.0 copy-done.3
  486.8 1.7 convolution_bitcast_fusion
  488.5 0.0 all-reduce.2.cloned.1.call-update
  488.5 0.8 copy.43.wg_ref
  489.4 8.4 %fusion = f32[]{:T(128)} fusion(bf16[8,512,768]{2,1,0:T(8,128)(2,1)} %res_ref.1, bf16[8,512,768]{2,1,0:T(8,128)(2,1)} %x_ref.1), kind=kLoop, calls=%fused_computation.1 | loop fusion | flops 12582911 | bytes 12582916 | tf_op jit(solution)/shard_map/gsh,gsh->/dot_general | solution.py:379
  497.8 15.5 %combine.1 = bf16[8,512,768]{2,1,0:T(8,128)(2,1)} custom-call(s32[8,1,512]{2,1,0:T(1,128)} %copy.36.l1_ref, s32[8,1,512]{2,1,0:T(1,128)} %broadcast_in_dim.19.l2_ref, bf16[4,16,8,16,768]{4,3,2,1,0:T(8,128)(2,1)} %bitcast.34, bf16[8,512,768]{2,1,0:T(8,128)(2,1)} %res_ref.1, bf16[8,512,64]{2,1,0:T(8,128)(2,1)} %copy-done.3, bf16[768,64]{1,0:T(8,128)(2,1)} %copy.43.wg_ref), custom_call_target="tpu_custom_call" | custom-call | flops 6442450944 | bytes 31457280 | tf_op jit(solution)/shard_map/combine/pallas_call | solution.py:324
  513.3 1.5 multiply_reduce_fusion.1
  516.1 32.3 %psum.14 = f32[1]{0:T(128)} all-reduce(f32[1]{0:T(128)} %bitcast.9), channel_id=1, replica_groups=mesh['ep'=16] {'ep'}, use_global_device_ids=true, to_apply=%region_10.11 | all-reduce | flops 1 | bytes 8 | tf_op jit(solution)/shard_map/psum | solution.py:392
  549.6 3.4 all-reduce.2.cloned.1.call-done
  553.1 16.7 %copy.64 = bf16[4,768,3072]{2,1,0:T(8,128)(2,1)} copy(bf16[4,768,3072]{2,1,0:T(8,128)(2,1)} %get-tuple-element.39) | data formatting | bytes 37748736
  569.8 16.7 %copy.65 = bf16[4,3072,768]{2,1,0:T(8,128)(2,1)} copy(bf16[4,3072,768]{2,1,0:T(8,128)(2,1)} %get-tuple-element.40) | data formatting | bytes 37748736
  586.5 0.7 copy.66
  (48 shorter events, 0.2 us)
Async XLA Ops:
  7.2 545.9 %all-reduce.2.cloned.1.call-start = ((), (), s32[]{:S(2)}) async-start(), calls=%async_computation | async-start | bytes 393216 | tf_op jit(solution)/shard_map/psum | solution.py:392
  12.0 4.6 copy-start.4
  12.0 0.7 copy-start.21
  12.0 0.7 copy-start.11
  12.7 3.9 copy-start.1
  12.8 3.9 copy-start.9
  16.7 7.2 %copy-start.7 = (f32[8,512]{1,0:T(8,128)}, f32[8,512]{1,0:T(8,128)S(1)}, u32[]{:S(2)}) copy-start(f32[8,512]{1,0:T(8,128)S(1)} %fusion.15) | copy-start | bytes 49156
  20.9 3.1 copy-start.17
  20.9 3.1 copy-start.19
  24.0 4.7 copy-start.22
  24.0 4.7 copy-start.24
  26.7 0.6 copy-start.13
  49.4 423.3 %copy-start.10 = (s32[8,512]{1,0:T(8,128)S(1)}, s32[8,512]{1,0:T(8,128)}, u32[]{:S(2)}) copy-start(s32[8,512]{1,0:T(8,128)} %param.14) | copy-start | bytes 49156
  49.4 423.3 %copy-start.23 = (s32[8,512]{1,0:T(8,128)S(1)}, s32[8,512]{1,0:T(8,128)}, u32[]{:S(2)}) copy-start(s32[8,512]{1,0:T(8,128)} %copy-done.22) | copy-start | bytes 49156
  49.4 424.3 %copy-start.12 = (s32[8,512]{1,0:T(8,128)S(1)}, s32[8,512]{1,0:T(8,128)}, u32[]{:S(2)}) copy-start(s32[8,512]{1,0:T(8,128)} %param.13) | copy-start | bytes 49156
  49.5 424.3 %copy-start.25 = (s32[8,512]{1,0:T(8,128)S(1)}, s32[8,512]{1,0:T(8,128)}, u32[]{:S(2)}) copy-start(s32[8,512]{1,0:T(8,128)} %copy-done.24) | copy-start | bytes 49156
  471.4 5.2 copy-start.18
  471.4 5.2 copy-start.20
  471.4 5.2 copy-start.2
  471.4 5.2 copy-start.5
  471.4 5.2 copy-start.8
  472.7 8.6 %copy-start.15 = (f32[64,8,16]{0,2,1:T(8,128)}, f32[64,8,16]{0,2,1:T(8,128)S(1)}, u32[]{:S(2)}) copy-start(f32[64,8,16]{0,2,1:T(8,128)S(1)} %copy.38) | copy-start | bytes 98308
  473.7 13.1 %copy-start = (bf16[8,512,768]{2,1,0:T(8,128)(2,1)S(1)}, bf16[8,512,768]{2,1,0:T(8,128)(2,1)}, u32[]{:S(2)}) copy-start(bf16[8,512,768]{2,1,0:T(8,128)(2,1)} %x_ref.1) | copy-start | bytes 18874372
  485.9 1.0 copy-start.3
  486.8 1.7 copy-start.6
  497.8 15.5 %copy-start.14 = (f32[64,8,16]{0,2,1:T(8,128)S(1)}, f32[64,8,16]{0,2,1:T(8,128)}, u32[]{:S(2)}) copy-start(f32[64,8,16]{0,2,1:T(8,128)} %copy-done.13) | copy-start | bytes 98308
  569.8 16.7 %copy-start.16 = (f32[768,64]{0,1:T(8,128)S(1)}, f32[768,64]{0,1:T(8,128)}, u32[]{:S(2)}) copy-start(f32[768,64]{0,1:T(8,128)} %all-reduce.2.cloned.1.call-done) | copy-start | bytes 589828
Sparse Core Ops, SparseCore 0:
  488.6 64.3 all-reduce.1

commit v2 on v1

--- a/solution.py
+++ b/solution.py
@@ -9,6 +9,7 @@
 
 ALPHA = 0.01
 SOURCES = 4
+LATE = 2
 ORDER = (14, 15, 1, 6, 7, 8, 9, 10, 11, 4, 5, 12, 13, 2, 3)
 FF_TILE = 768
 VMEM_LIMIT = 64 * 1024 * 1024 - 128 * 1024
@@ -41,40 +42,14 @@
     return first_hot, second_hot, first_count, slot_first, slot_second
 
 
-def dispatch_body(l1_ref, l2_ref, x_ref, r_ref, out_ref):
-    local, devices, _, _, cap_rows, hidden = out_ref.shape
-    slots, seq_len = devices * cap_rows, x_ref.shape[1]
-    ids = lax.broadcasted_iota(jnp.int32, (slots, seq_len), 0)
-    for j in range(local):
-        hit = (l1_ref[0] - j * slots == ids) | (l2_ref[0] - j * slots == ids)
-        hot = jnp.where(hit, 1.0, 0.0).astype(BF16)
-        for k, ref in enumerate((x_ref, r_ref)):
-            out_ref[j, :, k, 0] = dot(hot, ref[0]).astype(BF16).reshape(devices, cap_rows, hidden)
-
-
-def dispatch(local, devices, cap_rows, l1, l2, x, r):
-    groups, seq_len, hidden = x.shape
-    slots = local * devices * cap_rows
-    id_spec = pl.BlockSpec((1, 1, seq_len), lambda g: (g, 0, 0))
-    row_spec = pl.BlockSpec((1, seq_len, hidden), lambda g: (g, 0, 0))
-    return pl.pallas_call(
-        dispatch_body,
-        out_shape=jax.ShapeDtypeStruct((local, devices, 2, groups, cap_rows, hidden), BF16),
-        grid=(groups,),
-        in_specs=[id_spec, id_spec, row_spec, row_spec],
-        out_specs=pl.BlockSpec((local, devices, 2, 1, cap_rows, hidden), lambda g: (0, 0, 0, g, 0, 0)),
-        compiler_params=pltpu.CompilerParams(dimension_semantics=('arbitrary',), vmem_limit_bytes=VMEM_LIMIT),
-        cost_estimate=pl.CostEstimate(flops=4 * groups * slots * seq_len * hidden, bytes_accessed=4 * x.size + 4 * groups * slots * hidden, transcendentals=0),
-        name='dispatch',
-    )(l1[:, None, :], l2[:, None, :], x, r)
-
-
-def moe_body(ff_tile, send_ref, nstat_ref, w1_ref, w2_ref, recv_ref, dxs_ref, back_ref, dw1_ref, dw2_ref, dsend_ref, dback_ref, stat_ref,
+def moe_body(ff_tile, l1_ref, l2_ref, xg_ref, rg_ref, nstat_ref, w1_ref, w2_ref, send_ref, recv_ref, dxs_ref, late_ref, back_ref, dw1_ref, dw2_ref, dsend_ref, dback_ref, stat_ref,
              w1_buf, w2_buf, acc1, acc2, tile, dx_tile, nrecv, dwin,
-             in_send, in_recv, out_send, out_recv, n_send, n_recv, d_send, d_recv, w_sem, x_sem, dx_sem, dw_sem, own_sem):
-    local, devices, both, hidden = send_ref.shape
-    window = both // 2
+             in_send, in_recv, out_send, out_recv, n_send, n_recv, d_send, d_recv, w_sem, x_sem, dx_sem, dw_sem, own_sem, load_sem):
+    local, devices, _, groups, cap_rows, hidden = send_ref.shape
+    window = groups * cap_rows
+    seq_len = xg_ref.shape[1]
     ff = w1_ref.shape[2]
+    early = dxs_ref.shape[0]
     rows = SOURCES * window
     tiles = devices // SOURCES
     me = lax.axis_index('ep')
@@ -145,8 +120,42 @@
     each_peer(lambda k, peer: n_copy(k, peer).start())
     own = pltpu.make_async_copy(nstat_ref.at[me], nrecv.at[me], own_sem)
     own.start()
-    for j in range(local):
+
+    held = w2_buf.shape[1] // seq_len
+    x_at = [w2_buf.at[g // held, pl.ds(g % held * seq_len, seq_len)] for g in range(groups)]
+    wide = ff // hidden
+    r_at = [w1_buf.at[g // wide, pl.ds(0, seq_len), pl.ds(g % wide * hidden, hidden)] for g in range(groups)]
+    loads = [(pltpu.make_async_copy(xg_ref.at[g], x_at[g], load_sem.at[g, 0]), pltpu.make_async_copy(rg_ref.at[g], r_at[g], load_sem.at[g, 1])) for g in range(groups)]
+    for pair in loads:
+        for copy in pair:
+            copy.start()
+    slots = devices * cap_rows
+    ids = lax.broadcasted_iota(jnp.int32, (slots, seq_len), 0)
+
+    @pl.loop(0, local)
+    def _(j):
+        def placed(g, k):
+            return pltpu.make_async_copy(dx_tile.at[g % 2, k], send_ref.at[j, :, k, g], dx_sem.at[g % 2 * 2 + k])
+
+        for g in range(groups):
+            @pl.when(j == 0)
+            def _():
+                for copy in loads[g]:
+                    copy.wait()
+
+            hit = (l1_ref[g] - j * slots == ids) | (l2_ref[g] - j * slots == ids)
+            hot = jnp.where(hit, 1.0, 0.0).astype(BF16)
+            for k, src in enumerate((x_at[g], r_at[g])):
+                value = dot(hot, src[...]).astype(BF16).reshape(devices, cap_rows, hidden)
+                if g >= 2:
+                    placed(g - 2, k).wait()
+                dx_tile[g % 2, k] = value
+                placed(g, k).start()
+        for g in (groups - 2, groups - 1):
+            for k in range(2):
+                placed(g, k).wait()
         start_in(j)
+
     for copy in weight_copies(0, 0):
         copy.start()
     own.wait()
@@ -195,8 +204,8 @@
         for p, (k, s) in enumerate(sources):
             tile_copy(j, s, p, recv_ref).wait()
 
-        x = tile[:, :window].reshape(rows, hidden)
-        r = tile[:, window:].reshape(rows, hidden).astype(F32)
+        x = tile[:, 0].reshape(rows, hidden)
+        r = tile[:, 1].reshape(rows, hidden).astype(F32)
         weights = [jnp.sum(jnp.where(diag, nrecv[s, pl.ds(j, 1), :], 0.0), axis=1, keepdims=True) for _, s in sources]
         g = (r * jnp.concatenate(weights, axis=0)).astype(BF16)
         h = None
@@ -218,32 +227,42 @@
             dx = dp if dx is None else dx + dp
             acc1[:, f0:f0 + ff_tile] += dot(x, gp, ((0,), (0,)))
             acc2[f0:f0 + ff_tile, :] += dot(act, g, ((0,), (0,)))
-        dx_tile[slot] = dx.astype(BF16).reshape(SOURCES, window, hidden)
-        stores = [pltpu.make_async_copy(dx_tile.at[slot, p], dxs_ref.at[j, s], dx_sem.at[p]) for p, (_, s) in enumerate(sources)]
-        for p, copy in enumerate(stores):
-            if p != 2:
-                copy.start()
-
-        @pl.when(t > 0)
-        def _():
-            stores[2].start()
-
-        @pl.when(t == 0)
-        def _():
-            kept = pltpu.make_async_copy(dx_tile.at[slot, 2], back_ref.at[j, me], dx_sem.at[2])
-            kept.start()
+        dx_tile[slot] = dx.astype(BF16).reshape(dx_tile.shape[1:])
+        def store(p, dst):
+            return pltpu.make_async_copy(dx_tile.at[slot, p // 2, pl.ds(p % 2 * groups, groups)], dst, dx_sem.at[p])
+
+        @pl.when(j < early)
+        def _():
+            for p, (_, s) in enumerate(sources):
+                if p == 2:
+                    @pl.when(t == 0)
+                    def _():
+                        store(p, back_ref.at[j, me]).start()
+
+                    @pl.when(t > 0)
+                    def _():
+                        store(p, dxs_ref.at[j, s]).start()
+                else:
+                    store(p, dxs_ref.at[j, s]).start()
+
+        @pl.when(j >= early)
+        def _():
+            for p, (_, s) in enumerate(sources):
+                store(p, late_ref.at[s, j - early]).start()
 
         d = jnp.sum(r * h.astype(BF16).astype(F32), axis=1, keepdims=True)
         for p, (_, s) in enumerate(sources):
             dwin[s, pl.ds(j, 1), :] = jnp.sum(jnp.where(diag, d[p * window:(p + 1) * window], 0.0), axis=0, keepdims=True)
         for p, (k, s) in enumerate(sources):
-            stores[p].wait()
+            store(p, late_ref.at[s, 0]).wait()
             if p == 2:
-                @pl.when(t > 0)
+                @pl.when((j < early) & (t > 0))
                 def _():
                     out_copy(j, k, s).start()
             else:
-                out_copy(j, k, s).start()
+                @pl.when(j < early)
+                def _():
+                    out_copy(j, k, s).start()
 
         @pl.when(t == tiles - 1)
         def _():
@@ -266,58 +285,68 @@
     @pl.loop(0, local)
     def _(j):
         each_peer(lambda k, peer: in_copy(j, k, peer).wait_send())
-        each_peer(lambda k, peer: out_landing(j, k, peer).wait())
-
-
-def moe(send, nstat, w_in, w_out):
-    local, devices, both, hidden = send.shape
-    window = both // 2
-    ff = w_in.shape[2]
+
+        @pl.when(j < early)
+        def _():
+            each_peer(lambda k, peer: out_landing(j, k, peer).wait())
+
+
+def moe(l1, l2, x, r, nstat, w_in, w_out, cap_rows):
+    local, hidden, ff = w_in.shape
+    devices = nstat.shape[0]
+    groups = x.shape[0]
+    early = local - LATE
     anywhere = pl.BlockSpec(memory_space=pl.ANY)
-    slots = jax.ShapeDtypeStruct((local, devices, window, hidden), BF16)
+    vmem = pl.BlockSpec(memory_space=pltpu.VMEM)
+    region = (groups, cap_rows, hidden)
+    send = jax.ShapeDtypeStruct((local, devices, 2) + region, BF16)
+    slots = jax.ShapeDtypeStruct((early, devices) + region, BF16)
+    late = jax.ShapeDtypeStruct((devices, LATE) + region, BF16)
     small = jax.ShapeDtypeStruct(nstat.shape, F32)
     dma = pltpu.SemaphoreType.DMA
+    rows = devices * groups * cap_rows
     return pl.pallas_call(
         functools.partial(moe_body, FF_TILE),
         out_shape=(
-            jax.ShapeDtypeStruct(send.shape, BF16), slots, slots,
+            send, send, slots, late, slots,
             jax.ShapeDtypeStruct(w_in.shape, BF16), jax.ShapeDtypeStruct(w_out.shape, BF16),
             small, small, jax.ShapeDtypeStruct(nstat.shape[1:], F32),
         ),
-        in_specs=[anywhere] * 4,
-        out_specs=(anywhere,) * 7 + (pl.BlockSpec(memory_space=pltpu.VMEM),),
+        in_specs=[vmem] * 2 + [anywhere] * 5,
+        out_specs=(anywhere,) * 9 + (vmem,),
         scratch_shapes=[
             pltpu.VMEM((2, hidden, ff), BF16), pltpu.VMEM((2, ff, hidden), BF16),
             pltpu.VMEM((hidden, ff), F32), pltpu.VMEM((ff, hidden), F32),
-            pltpu.VMEM((SOURCES, both, hidden), BF16), pltpu.VMEM((2, SOURCES, window, hidden), BF16),
+            pltpu.VMEM((SOURCES, 2) + region, BF16), pltpu.VMEM((2, 2, devices, cap_rows, hidden), BF16),
             pltpu.VMEM(nstat.shape, F32), pltpu.VMEM(nstat.shape, F32),
-            dma((local, devices)), dma((local, devices)), dma((local, devices)), dma((local, devices)),
+            dma((local, devices)), dma((local, devices)), dma((early, devices)), dma((early, devices)),
             dma((devices,)), dma((devices,)), dma((devices,)), dma((devices,)),
-            dma((2, 2)), dma((SOURCES,)), dma((SOURCES,)), dma((2, 2)), dma,
+            dma((2, 2)), dma((SOURCES,)), dma((SOURCES,)), dma((2, 2)), dma, dma((groups, 2)),
         ],
         compiler_params=pltpu.CompilerParams(has_side_effects=True, vmem_limit_bytes=VMEM_LIMIT),
-        cost_estimate=pl.CostEstimate(flops=12 * local * devices * window * hidden * ff, bytes_accessed=8 * local * hidden * ff, transcendentals=local * devices * window * ff),
+        cost_estimate=pl.CostEstimate(flops=12 * local * rows * hidden * ff, bytes_accessed=8 * local * hidden * ff, transcendentals=local * rows * ff),
         name='moe',
-    )(send, nstat, w_in, w_out)
-
-
-def combine_body(l1_ref, l2_ref, back_ref, res_ref, gl_ref, wg_ref, out_ref):
-    local, devices, _, cap_rows, hidden = back_ref.shape
+    )(l1[:, None, :], l2[:, None, :], x, r, nstat, w_in, w_out)
+
+
+def combine_body(l1_ref, l2_ref, early_ref, late_ref, res_ref, gl_ref, wg_ref, out_ref):
+    early, devices, _, cap_rows, hidden = early_ref.shape
     seq_len = l1_ref.shape[2]
-    slots = local * devices * cap_rows
+    slots = devices * cap_rows
     ids = lax.broadcasted_iota(jnp.int32, (slots, seq_len), 0)
-    hit = (l1_ref[0] == ids) | (l2_ref[0] == ids)
-    hot = jnp.where(hit, 1.0, 0.0).astype(BF16)
-    total = dot(hot, back_ref[...].reshape(slots, hidden), ((0,), (0,)))
-    total += res_ref[0].astype(F32)
-    total += dot(gl_ref[0], wg_ref[...], ((1,), (1,)))
+    total = res_ref[0].astype(F32) + dot(gl_ref[0], wg_ref[...], ((1,), (1,)))
+    for j in range(early + late_ref.shape[1]):
+        hit = (l1_ref[0] - j * slots == ids) | (l2_ref[0] - j * slots == ids)
+        hot = jnp.where(hit, 1.0, 0.0).astype(BF16)
+        back = early_ref[j] if j < early else late_ref[:, j - early]
+        total += dot(hot, back.reshape(slots, hidden), ((0,), (0,)))
     out_ref[0] = total.astype(out_ref.dtype)
 
 
-def combine(l1, l2, back, res, grad_logits, w_gate):
+def combine(l1, l2, early, late, res, grad_logits, w_gate):
     groups, seq_len, hidden = res.shape
-    local, devices, _, cap_rows, _ = back.shape
-    slots = local * devices * cap_rows
+    devices, count, _, cap_rows, _ = late.shape
+    slots = (early.shape[0] + count) * devices * cap_rows
     experts = w_gate.shape[1]
     id_spec = pl.BlockSpec((1, 1, seq_len), lambda g: (g, 0, 0))
     row_spec = pl.BlockSpec((1, seq_len, hidden), lambda g: (g, 0, 0))
@@ -326,14 +355,74 @@
         out_shape=jax.ShapeDtypeStruct(res.shape, BF16),
         grid=(groups,),
         in_specs=[
-            id_spec, id_spec, pl.BlockSpec((local, devices, 1, cap_rows, hidden), lambda g: (0, 0, g, 0, 0)), row_spec,
-            pl.BlockSpec((1, seq_len, experts), lambda g: (g, 0, 0)), pl.BlockSpec((hidden, experts), lambda g: (0, 0)),
+            id_spec, id_spec,
+            pl.BlockSpec((early.shape[0], devices, 1, cap_rows, hidden), lambda g: (0, 0, g, 0, 0)),
+            pl.BlockSpec((devices, count, 1, cap_rows, hidden), lambda g: (0, 0, g, 0, 0)),
+            row_spec, pl.BlockSpec((1, seq_len, experts), lambda g: (g, 0, 0)), pl.BlockSpec((hidden, experts), lambda g: (0, 0)),
         ],
         out_specs=row_spec,
         compiler_params=pltpu.CompilerParams(dimension_semantics=('arbitrary',), vmem_limit_bytes=VMEM_LIMIT),
         cost_estimate=pl.CostEstimate(flops=2 * groups * slots * seq_len * hidden, bytes_accessed=2 * groups * slots * hidden + 6 * res.size, transcendentals=0),
         name='combine',
-    )(l1[:, None, :], l2[:, None, :], back, res, grad_logits, w_gate)
+    )(l1[:, None, :], l2[:, None, :], early, late, res, grad_logits, w_gate)
+
+
+def copy_body(a_ref, b_ref, a_out, b_out):
+    a_out[...] = a_ref[...]
+    b_out[...] = b_ref[...]
+
+
+def settle(a, b):
+    cuts = 4
+    local = a.shape[0]
+    specs = [pl.BlockSpec((1, v.shape[1] // cuts, v.shape[2]), lambda j, q: (j, q, 0)) for v in (a, b)]
+    return pl.pallas_call(
+        copy_body,
+        out_shape=tuple(jax.ShapeDtypeStruct(v.shape, v.dtype) for v in (a, b)),
+        grid=(local, cuts),
+        in_specs=specs,
+        out_specs=tuple(specs),
+        compiler_params=pltpu.CompilerParams(dimension_semantics=('arbitrary', 'arbitrary'), vmem_limit_bytes=32 * 1024 * 1024),
+        cost_estimate=pl.CostEstimate(flops=1 << 34, bytes_accessed=4 * (a.size + b.size), transcendentals=0),
+        name='settle',
+    )(a, b)
+
+
+def reduce_body(part_ref, out_ref, landed, total, send1, recv1, send2, recv2):
+    devices = part_ref.shape[0]
+    me = lax.axis_index('ep')
+
+    def hop(src, dst, s, r, peer):
+        return pltpu.make_async_remote_copy(src_ref=src, dst_ref=dst, send_sem=s, recv_sem=r, device_id=(peer,), device_id_type=pl.DeviceIdType.MESH)
+
+    peers = [(k, lax.rem(me + k, devices), lax.rem(me - k + devices, devices)) for k in range(1, devices)]
+    for k, to, _ in peers:
+        hop(part_ref.at[to], landed.at[me], send1.at[k], recv1.at[k], to).start()
+    landed[me] = part_ref[me]
+    for k, to, source in peers:
+        hop(part_ref.at[to], landed.at[source], send1.at[k], recv1.at[k], to).wait()
+    value = jnp.sum(landed[...], axis=0)
+    total[...] = value
+    out_ref[me] = value
+    for k, to, _ in peers:
+        hop(total, out_ref.at[me], send2.at[k], recv2.at[k], to).start()
+    for k, to, source in peers:
+        hop(total, out_ref.at[source], send2.at[k], recv2.at[k], to).wait()
+
+
+def all_reduce(part):
+    dma = pltpu.SemaphoreType.DMA((part.shape[0],))
+    vmem = pl.BlockSpec(memory_space=pltpu.VMEM)
+    return pl.pallas_call(
+        reduce_body,
+        out_shape=jax.ShapeDtypeStruct(part.shape, F32),
+        in_specs=[vmem],
+        out_specs=vmem,
+        scratch_shapes=[pltpu.VMEM(part.shape, F32), pltpu.VMEM(part.shape[1:], F32), dma, dma, dma, dma],
+        compiler_params=pltpu.CompilerParams(has_side_effects=True, vmem_limit_bytes=16 * 1024 * 1024),
+        cost_estimate=pl.CostEstimate(flops=1 << 22, bytes_accessed=4 * part.size, transcendentals=0),
+        name='all_reduce',
+    )(part)
 
 
 def solution(mesh):
@@ -354,7 +443,6 @@
             return jnp.where(slot >= 0, ((expert_of % local) * ep_size + expert_of // local) * cap_rows + slot, -1)
 
         l1, l2 = slot_of(slot_first, first_ids), slot_of(slot_second, second_ids)
-        send = dispatch(local, ep_size, cap_rows, l1, l2, x_loc, r_loc).reshape(local, ep_size, 2 * region, hidden)
 
         logits = jnp.einsum('gsh,he->gse', x_loc, w_gate, preferred_element_type=F32)
         router_prob = jax.nn.softmax(logits, axis=-1)
@@ -372,7 +460,8 @@
         nwin_rows = nwin.reshape(ep_size, local, region)
         stat_rows = jnp.broadcast_to(jnp.pad(stats, (0, region - 2 * experts)), (ep_size, 1, region))
         nstat = jnp.concatenate([nwin_rows, stat_rows, jnp.zeros((ep_size, 7 - local, region), F32)], axis=1)
-        _, _, back, dw1, dw2, _, dback, stats = moe(send, nstat, w_in_loc, w_out_loc)
+        _, _, _, late, back, dw1, dw2, _, dback, stats = moe(l1, l2, x_loc, r_loc, nstat, w_in_loc, w_out_loc, cap_rows)
+        late = lax.all_to_all(late.reshape(ep_size, LATE * region, hidden), 'ep', 0, 0, tiled=True)
         frac_first = stats[local, :experts] / tokens_all
         mean_prob = stats[local, experts:2 * experts] / tokens_all
         dwin = dback[:, :local].reshape(experts, local_groups, cap_rows)
@@ -388,11 +477,18 @@
         grad_prob = grad_gate_first[..., None] * first_hot + grad_gate_second[..., None] * second_hot + (ALPHA * hidden * experts) * frac_first
         grad_logits = router_prob * (grad_prob - jnp.sum(router_prob * grad_prob, axis=-1, keepdims=True))
         grad_logits_bf = grad_logits.astype(BF16)
-        grad_gate_local = jnp.einsum('gsh,gse->he', x_loc, grad_logits_bf, preferred_element_type=F32)
-        grad_gate_w, dot_all = lax.psum((grad_gate_local, dot_sum[None]), 'ep')
-        loss_value = dot_all[0] / numel + ALPHA * experts * jnp.sum(frac_first * mean_prob)
-
-        grad_x = combine(l1, l2, back.reshape(local, ep_size, local_groups, cap_rows, hidden), r_loc, grad_logits_bf, w_gate)
+        grad_gate_local = jnp.einsum('gse,gsh->eh', grad_logits_bf, x_loc, preferred_element_type=F32)
+        lanes = 128
+        slice_rows = experts * hidden // (ep_size * lanes)
+        part = jnp.concatenate([grad_gate_local.reshape(ep_size, slice_rows, lanes), jnp.full((ep_size, 8, lanes), dot_sum)], axis=1)
+        dw1, dw2 = settle(dw1, dw2)
+        part, late = lax.optimization_barrier((part, late))
+        whole = all_reduce(part)
+        grad_gate_w = whole[:, :slice_rows].reshape(experts, hidden).T
+        loss_value = whole[0, slice_rows, 0] / numel + ALPHA * experts * jnp.sum(frac_first * mean_prob)
+
+        grad_x = combine(l1, l2, back, late.reshape(ep_size, LATE, local_groups, cap_rows, hidden),
+                         r_loc, grad_logits_bf, w_gate)
         return loss_value, grad_x, dw1, dw2, grad_gate_w
 
     row_spec = P('ep', None, None)

time: 597 us -> 515 us (0.86)
  Pallas kernels: 457 us -> 424 us
  blocking collectives: 32.3 us -> 0 us
  local copies, waits for them, and re-layouts: 39.8 us -> 12.5 us
  waiting for transfers between devices: 3.46 us -> 27.1 us
  between operations: 18.1 us -> 4.86 us
    pallas_call x2 -> x3, Pallas kernels: 442 us -> 409 us  [the longest x1 372 us: moe(): pl.pallas_call(functools.partial(moe_body, FF_TILE), out_shape=(send, sen...]
    psum x1 -> x0, blocking collectives: 32.3 us -> none  [layer_body(): grad_gate_w, dot_all = lax.psum((grad_gate_local, dot_sum[None]), 'ep')]
    unnamed x56 -> x53, local copies, waits for them, and re-layouts: 36.4 us -> 8.72 us
    all_to_all x0 -> x1, waiting for transfers between devices: none -> 27.1 us  [layer_body(): lax.all_to_all(late.reshape(ep_size, LATE * region, hidden), 'ep', 0, 0,...]
  transfers between devices with their start and end apart: 1 -> 1, of which waited for: 1 -> 1; matrix products, arithmetic and copies ran while one was open for 2% -> 5% of each run, Pallas kernels for 3% -> 4%
where the time goes in v2:
time: 515 us; the launch traced here: 513 us
  Pallas kernels  424 us (82%)
  waiting for transfers between devices  27.1 us (5%)
  other arithmetic  26.1 us (5%)
  matrix products  15.8 us (3%)
  local copies, waits for them, and re-layouts  12.5 us (2%)
    pallas_call x1, Pallas kernels, moe(): pl.pallas_call(functools.partial(moe_body, FF_TILE), out_shape=(send, sen...  372 us
    all_to_all x1, waiting for transfers between devices, layer_body(): lax.all_to_all(late.reshape(ep_size, LATE * region, hidden), 'ep', 0, 0,...  27.1 us
    pallas_call x1, Pallas kernels, settle(): pl.pallas_call(copy_body, out_shape=tuple((jax.ShapeDtypeStruct(v.shape,...  20.6 us
    pallas_call x1, Pallas kernels, all_reduce(): pl.pallas_call(reduce_body, out_shape=jax.ShapeDtypeStruct(part.shape, F3...  15.9 us
    pallas_call x1, Pallas kernels, combine(): pl.pallas_call(combine_body, out_shape=jax.ShapeDtypeStruct(res.shape, BF...  15 us
  transfers between devices with their start and end apart: 1, of which 1 were waited for; matrix products, arithmetic and copies ran while one was open for 5% of the time, Pallas kernels for 4%

profile of v2, /device:TPU:0, one launch (start us, length us, event | category | flops | bytes accessed | tf_op | source)
XLA Modules:
  0.0 513.5 jit_solution(13810838187710767019)
XLA Ops:
  0.6 4.8 fusion.74
  5.4 0.0 copy-start.20
  5.5 0.0 copy-start.12
  5.5 0.6 copy.29
  6.1 0.1 copy-done.20
  6.2 0.0 copy-done.12
  6.2 2.5 fusion.5
  8.7 1.3 fusion.15
  10.1 4.2 fusion.6
  14.3 0.0 copy-start.18
  14.4 3.0 fusion.1
  17.5 1.3 fusion.8
  18.8 1.3 fusion.21
  20.1 0.2 copy.36
  20.3 0.1 reshape.91
  20.4 0.3 copy-done.14
  20.7 0.6 broadcast_in_dim.17.l2_ref
  21.3 0.6 copy.37.l1_ref
  22.0 0.1 pad_maximum_fusion
  22.0 0.1 pad.3.clone
  22.1 0.7 maximum_maximum_fusion.nstat_ref
  22.8 372.1 %moe.1 = (bf16[4,16,2,8,16,768]{5,4,3,2,1,0:T(8,128)(2,1)}, bf16[4,16,2,8,16,768]{5,4,3,2,1,0:T(8,128)(2,1)}, bf16[2,16,8,16,768]{4,3,2,1,0:T(8,128)(2,1)}, bf16...) custom-call(s32[8,1,512]{2,1,0:T(1,128)} %copy.37.l1_ref, ...), custom_call_target="tpu_custom_call" | custom-call | flops 231928233984 | bytes 75497472 | tf_op jit(solution)/shard_map/moe/pallas_call | solution.py:308
  395.0 0.0 copy-start.7
  395.0 0.0 copy-start.11
  395.0 3.5 all-to-all-start
  398.5 0.0 copy-start.13
  398.6 0.0 copy-start.19
  398.6 0.0 copy-start.3
  398.6 0.8 copy.44.wg_ref
  399.4 0.1 reshape.92
  399.6 0.1 copy.38
  399.7 1.4 multiply_reduce_fusion.2
  401.1 1.0 fusion.18
  402.1 0.0 copy-start.1
  402.1 1.0 fusion.19
  403.2 4.7 multiply_reduce_fusion
  407.9 4.5 multiply_convert_fusion.gl_ref
  412.4 1.0 copy-done.4
  413.4 1.0 convolution_bitcast_fusion
  414.5 0.6 multiply_reduce_fusion.1
  415.1 8.4 %fusion = f32[]{:T(128)} fusion(bf16[8,512,768]{2,1,0:T(8,128)(2,1)} %res_ref.1, bf16[8,512,768]{2,1,0:T(8,128)(2,1)} %xg_ref.1), kind=kLoop, calls=%fused_computation.1 | loop fusion | flops 12582911 | bytes 12582916 | tf_op jit(solution)/shard_map/gsh,gsh->/dot_general | solution.py:468
  425.5 6.4 %copy-done = bf16[4,768,3072]{2,1,0:T(8,128)(2,1)S(1)} copy-done((bf16[4,768,3072]{2,1,0:T(8,128)(2,1)S(1)}, bf16[4,768,3072]{2,1,0:T(8,128)(2,1)}, u32[]{:S(2)}) %copy-start) | copy-done | bytes 18874392
  431.9 20.6 %settle.1 = (bf16[4,768,3072]{2,1,0:T(8,128)(2,1)}, bf16[4,3072,768]{2,1,0:T(8,128)(2,1)}) custom-call(bf16[4,768,3072]{2,1,0:T(8,128)(2,1)S(1)} %copy-done, bf16[4,3072,768]{2,1,0:T(8,128)(2,1)} %get-tuple-element.22.b_ref), custom_call_target="tpu_custom_call" | custom-call | flops 17179869184 | bytes 75497472 | tf_op jit(solution)/shard_map/settle/pallas_call | solution.py:379
  452.4 27.1 %all-to-all-done = bf16[16,256,768]{2,1,0:T(8,128)(2,1)} async-done(((bf16[16,256,768]{2,1,0:T(8,128)(2,1)}), bf16[16,256,768]{2,1,0:T(8,128)(2,1)}, u32[]{:S(2)}, u32[]{:S(2)}) %all-to-all-start) | async-done | bytes 6291488 | tf_op jit(solution)/shard_map/all_to_all | solution.py:464
  479.5 15.9 %all_reduce.1 = f32[16,32,128]{2,1,0:T(8,128)S(1)} custom-call(f32[16,32,128]{2,1,0:T(8,128)S(1)} %concatenate.11.part_ref), custom_call_target="tpu_custom_call" | custom-call | flops 4194304 | bytes 262144 | tf_op jit(solution)/shard_map/all_reduce/pallas_call | solution.py:416
  495.5 0.5 slice.17
  496.0 0.7 reshape.96
  497.4 15.0 %combine.1 = bf16[8,512,768]{2,1,0:T(8,128)(2,1)} custom-call(s32[8,1,512]{2,1,0:T(1,128)} %copy.37.l1_ref, s32[8,1,512]{2,1,0:T(1,128)} %broadcast_in_dim.17.l2_ref, bf16[2,16,8,16,768]{4,3,2,1,0:T(8,128)(2,1)} %get-tuple-element.19.early_ref, bf16[16,2,8,16,768]{4,3,2,1,0:T(8,128)(2,1)} %bitcast.12.late_ref, bf16[8,512,768]{2,1,0:T(8,128)(2,1)} %res_ref.1, ...), custom_call_target="tpu_custom_call" | custom-call | flops 6442450944 | bytes 31457280 | tf_op jit(solution)/shard_map/combine/pallas_call | solution.py:353
  (49 shorter events, 0.2 us)
Async XLA Ops:
  5.4 4.6 copy-start.5
  5.4 0.7 copy-start.20
  5.5 0.7 copy-start.12
  6.2 3.9 copy-start.2
  6.2 3.9 copy-start.10
  10.1 7.2 %copy-start.8 = (f32[8,512]{1,0:T(8,128)}, f32[8,512]{1,0:T(8,128)S(1)}, u32[]{:S(2)}) copy-start(f32[8,512]{1,0:T(8,128)S(1)} %fusion.15) | copy-start | bytes 49156
  14.3 3.1 copy-start.16
  14.3 3.1 copy-start.18
  17.4 4.7 copy-start.21
  17.4 4.7 copy-start.24
  20.1 0.6 copy-start.14
  395.0 3.6 copy-start.7
  395.0 4.5 copy-start.23
  395.0 6.2 %copy-start.11 = (s32[8,512]{1,0:T(8,128)S(1)}, s32[8,512]{1,0:T(8,128)}, u32[]{:S(2)}) copy-start(s32[8,512]{1,0:T(8,128)} %param.14) | copy-start | bytes 49156
  395.0 6.2 %copy-start.22 = (s32[8,512]{1,0:T(8,128)S(1)}, s32[8,512]{1,0:T(8,128)}, u32[]{:S(2)}) copy-start(s32[8,512]{1,0:T(8,128)} %copy-done.21) | copy-start | bytes 49156
  395.0 7.1 %copy-start.25 = (s32[8,512]{1,0:T(8,128)S(1)}, s32[8,512]{1,0:T(8,128)}, u32[]{:S(2)}) copy-start(s32[8,512]{1,0:T(8,128)} %copy-done.24) | copy-start | bytes 49156
  395.0 84.5 %all-to-all-start = ((bf16[16,256,768]{2,1,0:T(8,128)(2,1)}), bf16[16,256,768]{2,1,0:T(8,128)(2,1)}, u32[]{:S(2)}, u32[]{:S(2)}) async-start(bf16[16,256,768]{2,1,0:T(8,128)(2,1)} %bitcast.32), calls=%async_computation | async-start | bytes 12582912 | tf_op jit(solution)/shard_map/all_to_all | solution.py:464
  398.5 3.6 copy-start.13
  398.6 4.6 copy-start.17
  398.6 4.6 copy-start.19
  398.6 4.6 copy-start.3
  398.6 4.6 copy-start.6
  398.6 4.6 copy-start.9
  402.1 11.3 %copy-start.1 = (bf16[8,512,768]{2,1,0:T(8,128)(2,1)S(1)}, bf16[8,512,768]{2,1,0:T(8,128)(2,1)}, u32[]{:S(2)}) copy-start(bf16[8,512,768]{2,1,0:T(8,128)(2,1)} %xg_ref.1) | copy-start | bytes 18874372
  412.4 1.0 copy-start.4
  413.4 1.0 copy-start.15
  425.5 6.4 %copy-start = (bf16[4,768,3072]{2,1,0:T(8,128)(2,1)S(1)}, bf16[4,768,3072]{2,1,0:T(8,128)(2,1)}, u32[]{:S(2)}) copy-start(bf16[4,768,3072]{2,1,0:T(8,128)(2,1)} %get-tuple-element.21.a_ref) | copy-start | bytes 56623108

commit v3 on v2

--- a/solution.py
+++ b/solution.py
@@ -40,6 +40,52 @@
     slot_first = jnp.where(pos_first < cap_rows, pos_first, -1)
     slot_second = jnp.where((keep_ids == 1) & (pos_second < cap_rows), pos_second, -1)
     return first_hot, second_hot, first_count, slot_first, slot_second
+
+
+def plan_body(local, cap_rows, x_ref, wg_ref, e1_ref, e2_ref, k2_ref, l1_ref, l2_ref, nw_ref, st_ref):
+    seq_len, experts = x_ref.shape[1], wg_ref.shape[1]
+    devices = experts // local
+    e1, e2, k2 = e1_ref[0], e2_ref[0], k2_ref[0]
+    logits = dot(wg_ref[...], x_ref[0], ((0,), (1,)))
+    top = jnp.exp(logits - jnp.max(logits, axis=0, keepdims=True))
+    prob = top / jnp.sum(top, axis=0, keepdims=True)
+    ids = lax.broadcasted_iota(jnp.int32, (experts, seq_len), 0)
+    hot1 = jnp.where(ids == e1, 1.0, 0.0)
+    hot2 = jnp.where(ids == e2, 1.0, 0.0)
+    kept2 = jnp.where((ids == e2) & (k2 == 1), 1.0, 0.0)
+    square = (seq_len, seq_len)
+    earlier = jnp.where(lax.broadcasted_iota(jnp.int32, square, 0) < lax.broadcasted_iota(jnp.int32, square, 1), 1.0, 0.0).astype(BF16)
+    count = jnp.sum(hot1, axis=1, keepdims=True)
+    pos1 = jnp.sum(dot(hot1.astype(BF16), earlier) * hot1, axis=0, keepdims=True).astype(jnp.int32)
+    pos2 = jnp.sum((dot(kept2.astype(BF16), earlier) + count) * hot2, axis=0, keepdims=True).astype(jnp.int32)
+    gate1 = jnp.sum(prob * hot1, axis=0, keepdims=True)
+    gate2 = jnp.sum(prob * hot2, axis=0, keepdims=True)
+    both = gate1 + gate2
+    rows = lax.broadcasted_iota(jnp.int32, (cap_rows, seq_len), 0)
+    at1 = jnp.where(rows == pos1, 1.0, 0.0).astype(BF16)
+    at2 = jnp.where((rows == pos2) & (k2 == 1), 1.0, 0.0).astype(BF16)
+    nw_ref[0] = dot((hot1 * (gate1 / both)).astype(BF16), at1, ((1,), (1,))) + dot((hot2 * (gate2 / both)).astype(BF16), at2, ((1,), (1,)))
+    lane = lax.broadcasted_iota(jnp.int32, st_ref.shape[1:], 1)
+    st_ref[0] = jnp.where(lane == 0, count, jnp.sum(prob, axis=1, keepdims=True))
+    l1_ref[0] = jnp.where(pos1 < cap_rows, (lax.rem(e1, local) * devices + e1 // local) * cap_rows + pos1, -1)
+    l2_ref[0] = jnp.where((pos2 < cap_rows) & (k2 == 1), (lax.rem(e2, local) * devices + e2 // local) * cap_rows + pos2, -1)
+
+
+def plan(local, cap_rows, x, w_gate, first_ids, second_ids, keep_ids):
+    groups, seq_len, hidden = x.shape
+    experts = w_gate.shape[1]
+    id_spec = pl.BlockSpec((1, 1, seq_len), lambda g: (g, 0, 0))
+    ids = jax.ShapeDtypeStruct((groups, 1, seq_len), jnp.int32)
+    return pl.pallas_call(
+        functools.partial(plan_body, local, cap_rows),
+        out_shape=(ids, ids, jax.ShapeDtypeStruct((groups, experts, cap_rows), F32), jax.ShapeDtypeStruct((groups, experts, 128), F32)),
+        grid=(groups,),
+        in_specs=[pl.BlockSpec((1, seq_len, hidden), lambda g: (g, 0, 0)), pl.BlockSpec((hidden, experts), lambda g: (0, 0)), id_spec, id_spec, id_spec],
+        out_specs=(id_spec, id_spec, pl.BlockSpec((1, experts, cap_rows), lambda g: (g, 0, 0)), pl.BlockSpec((1, experts, 128), lambda g: (g, 0, 0))),
+        compiler_params=pltpu.CompilerParams(dimension_semantics=('arbitrary',), vmem_limit_bytes=VMEM_LIMIT),
+        cost_estimate=pl.CostEstimate(flops=1 << 32, bytes_accessed=2 * x.size, transcendentals=groups * seq_len * experts),
+        name='plan',
+    )(x, w_gate, first_ids[:, None, :], second_ids[:, None, :], keep_ids[:, None, :])
 
 
 def moe_body(ff_tile, l1_ref, l2_ref, xg_ref, rg_ref, nstat_ref, w1_ref, w2_ref, send_ref, recv_ref, dxs_ref, late_ref, back_ref, dw1_ref, dw2_ref, dsend_ref, dback_ref, stat_ref,
@@ -326,7 +372,7 @@
         compiler_params=pltpu.CompilerParams(has_side_effects=True, vmem_limit_bytes=VMEM_LIMIT),
         cost_estimate=pl.CostEstimate(flops=12 * local * rows * hidden * ff, bytes_accessed=8 * local * hidden * ff, transcendentals=local * rows * ff),
         name='moe',
-    )(l1[:, None, :], l2[:, None, :], x, r, nstat, w_in, w_out)
+    )(l1, l2, x, r, nstat, w_in, w_out)
 
 
 def combine_body(l1_ref, l2_ref, early_ref, late_ref, res_ref, gl_ref, wg_ref, out_ref):
@@ -364,7 +410,7 @@
         compiler_params=pltpu.CompilerParams(dimension_semantics=('arbitrary',), vmem_limit_bytes=VMEM_LIMIT),
         cost_estimate=pl.CostEstimate(flops=2 * groups * slots * seq_len * hidden, bytes_accessed=2 * groups * slots * hidden + 6 * res.size, transcendentals=0),
         name='combine',
-    )(l1[:, None, :], l2[:, None, :], early, late, res, grad_logits, w_gate)
+    )(l1, l2, early, late, res, grad_logits, w_gate)
 
 
 def copy_body(a_ref, b_ref, a_out, b_out):
@@ -437,14 +483,20 @@
         tokens_all = local_groups * ep_size * seq_len
         numel = tokens_all * hidden
 
+        l1, l2, nwin, marks = plan(local, cap_rows, x_loc, w_gate, first_ids, second_ids, keep_ids)
+        nwin = nwin.transpose(1, 0, 2)
+        stats = jnp.sum(marks[:, :, :2], axis=0).T.reshape(-1)
+        nwin_rows = nwin.reshape(ep_size, local, region)
+        stat_rows = jnp.broadcast_to(jnp.pad(stats, (0, region - 2 * experts)), (ep_size, 1, region))
+        nstat = jnp.concatenate([nwin_rows, stat_rows, jnp.zeros((ep_size, 7 - local, region), F32)], axis=1)
+        _, _, _, late, back, dw1, dw2, _, dback, stats = moe(l1, l2, x_loc, r_loc, nstat, w_in_loc, w_out_loc, cap_rows)
+        late = lax.all_to_all(late.reshape(ep_size, LATE * region, hidden), 'ep', 0, 0, tiled=True)
+        frac_first = stats[local, :experts] / tokens_all
+        mean_prob = stats[local, experts:2 * experts] / tokens_all
+        dwin = dback[:, :local].reshape(experts, local_groups, cap_rows)
+        first_ids, second_ids, keep_ids, gate_late, dwin = lax.optimization_barrier((first_ids, second_ids, keep_ids, w_gate, dwin))
         first_hot, second_hot, first_count, slot_first, slot_second = route(first_ids, second_ids, keep_ids, experts, cap_rows)
-
-        def slot_of(slot, expert_of):
-            return jnp.where(slot >= 0, ((expert_of % local) * ep_size + expert_of // local) * cap_rows + slot, -1)
-
-        l1, l2 = slot_of(slot_first, first_ids), slot_of(slot_second, second_ids)
-
-        logits = jnp.einsum('gsh,he->gse', x_loc, w_gate, preferred_element_type=F32)
+        logits = jnp.einsum('gsh,he->gse', x_loc, gate_late, preferred_element_type=F32)
         router_prob = jax.nn.softmax(logits, axis=-1)
         gate_first = jnp.sum(router_prob * first_hot, axis=-1)
         gate_second = jnp.sum(router_prob * second_hot, axis=-1)
@@ -454,17 +506,6 @@
         slot_ids = jnp.arange(cap_rows, dtype=jnp.int32)
         slot_hot_first = (slot_first[..., None] == slot_ids).astype(BF16)
         slot_hot_second = (slot_second[..., None] == slot_ids).astype(BF16)
-        nwin = (jnp.einsum('gse,gsc->egc', first_hot, slot_hot_first * norm_first[..., None], preferred_element_type=F32)
-                + jnp.einsum('gse,gsc->egc', second_hot, slot_hot_second * norm_second[..., None], preferred_element_type=F32))
-        stats = jnp.concatenate([jnp.sum(first_count, axis=0), jnp.sum(router_prob, axis=(0, 1))])
-        nwin_rows = nwin.reshape(ep_size, local, region)
-        stat_rows = jnp.broadcast_to(jnp.pad(stats, (0, region - 2 * experts)), (ep_size, 1, region))
-        nstat = jnp.concatenate([nwin_rows, stat_rows, jnp.zeros((ep_size, 7 - local, region), F32)], axis=1)
-        _, _, _, late, back, dw1, dw2, _, dback, stats = moe(l1, l2, x_loc, r_loc, nstat, w_in_loc, w_out_loc, cap_rows)
-        late = lax.all_to_all(late.reshape(ep_size, LATE * region, hidden), 'ep', 0, 0, tiled=True)
-        frac_first = stats[local, :experts] / tokens_all
-        mean_prob = stats[local, experts:2 * experts] / tokens_all
-        dwin = dback[:, :local].reshape(experts, local_groups, cap_rows)
         dot_sum = jnp.einsum('gsh,gsh->', x_loc, r_loc, preferred_element_type=F32) + jnp.sum(nwin * dwin)
         dwin_bf = dwin.astype(BF16)
         d_first = jnp.einsum('gse,egc->gsc', first_hot, dwin_bf, preferred_element_type=F32)

time: 515 us -> 511 us (level)
  waiting for transfers between devices: 27.1 us -> 13.1 us
  Pallas kernels: 424 us -> 433 us
    all_to_all x1, waiting for transfers between devices: 27.1 us -> 13.1 us  [layer_body(): lax.all_to_all(late.reshape(ep_size, LATE * region, hidden), 'ep', 0, 0,...]
    pallas_call x0 -> x1, Pallas kernels: none -> 9.12 us  [plan(): pl.pallas_call(functools.partial(plan_body, local, cap_rows), out_shape=(...]
  transfers between devices with their start and end apart: 1 -> 1, of which waited for: 1 -> 1; matrix products, arithmetic and copies ran while one was open for 5% -> 7% of each run, Pallas kernels for 4% -> 4%
where the time goes in v3:
time: 511 us; the launch traced here: 509 us
  Pallas kernels  433 us (85%)
  other arithmetic  26.1 us (5%)
  local copies, waits for them, and re-layouts  16.1 us (3%)
  waiting for transfers between devices  13.1 us (3%)
  matrix products  13 us (3%)
    pallas_call x1, Pallas kernels, moe(): pl.pallas_call(functools.partial(moe_body, FF_TILE), out_shape=(send, sen...  372 us
    pallas_call x1, Pallas kernels, settle(): pl.pallas_call(copy_body, out_shape=tuple((jax.ShapeDtypeStruct(v.shape,...  20.6 us
    pallas_call x1, Pallas kernels, all_reduce(): pl.pallas_call(reduce_body, out_shape=jax.ShapeDtypeStruct(part.shape, F3...  15.9 us
    pallas_call x1, Pallas kernels, combine(): pl.pallas_call(combine_body, out_shape=jax.ShapeDtypeStruct(res.shape, BF...  14.9 us
    all_to_all x1, waiting for transfers between devices, layer_body(): lax.all_to_all(late.reshape(ep_size, LATE * region, hidden), 'ep', 0, 0,...  13.1 us
  transfers between devices with their start and end apart: 1, of which 1 were waited for; matrix products, arithmetic and copies ran while one was open for 7% of the time, Pallas kernels for 4%

profile of v3, /device:TPU:0, one launch (start us, length us, event | category | flops | bytes accessed | tf_op | source)
XLA Modules:
  0.0 509.2 jit_solution(7739905820908566238)
XLA Ops:
  0.6 1.7 copy.40.wg_ref
  2.3 1.3 broadcast_in_dim.15.e1_ref
  3.7 1.3 broadcast_in_dim.16.e2_ref
  5.0 1.3 broadcast_in_dim.17.k2_ref
  6.3 9.1 %plan.1 = (s32[8,1,512]{2,1,0:T(1,128)}, s32[8,1,512]{2,1,0:T(1,128)}, f32[8,64,16]{2,1,0:T(8,128)}, f32[8,64,128]{2,1,0:T(8,128)}) custom-call(bf16[8,512,768]{2,1,0:T(8,128)(2,1)} %xg_ref.1, bf16[768,64]{1,0:T(8,128)(2,1)} %copy.40.wg_ref, s32[8,1,512]{2,1,0:T(1,128)} %broadcast_in_dim.15.e1_ref, s32[8,1,512]{2,1,0:T(1,128)} %broadcast_in_dim.16.e2_ref, ...), custom_call_target="tpu_custom_call" | custom-call | flops 4294967296 | bytes 6291456 | tf_op jit(solution)/shard_map/plan/pallas_call | solution.py:79
  15.4 1.1 copy.41
  16.6 0.1 reshape.82
  16.7 1.0 slice_reduce_fusion
  17.7 0.1 copy.42
  17.7 0.1 reshape.83
  17.8 0.1 pad.3.clone
  17.9 0.7 maximum_maximum_fusion.nstat_ref
  18.6 372.1 %moe.1 = (bf16[4,16,2,8,16,768]{5,4,3,2,1,0:T(8,128)(2,1)}, bf16[4,16,2,8,16,768]{5,4,3,2,1,0:T(8,128)(2,1)}, bf16[2,16,8,16,768]{4,3,2,1,0:T(8,128)(2,1)}, bf16...) custom-call(s32[8,1,512]{2,1,0:T(1,128)} %get-tuple-element.24.l1_re, ...), custom_call_target="tpu_custom_call" | custom-call | flops 231928233984 | bytes 75497472 | tf_op jit(solution)/shard_map/moe/pallas_call | solution.py:354
  390.7 0.0 copy-start.7
  390.7 0.0 copy-start.3
  390.7 3.5 all-to-all-start
  394.2 0.0 copy-done.7
  394.3 0.1 reshape.84
  394.4 0.0 copy-done.3
  394.4 4.6 fusion.35
  399.0 0.0 copy-start.6
  399.0 0.0 copy-start.4
  399.1 0.0 copy-start.5
  399.1 2.0 fusion.39
  401.1 0.1 copy.45
  401.2 1.4 multiply_reduce_fusion.1
  402.7 0.0 copy-done.5
  402.7 3.6 fusion.3
  406.3 0.0 slice-start
  406.3 3.0 fusion.2
  409.3 1.0 fusion.20
  410.3 0.0 slice-start.1
  410.3 2.5 fusion.6
  412.9 1.0 fusion.21
  413.9 4.2 multiply_reduce_fusion
  418.1 4.0 multiply_convert_fusion.gl_ref
  422.1 1.0 copy-done.1
  423.1 0.0 slice-done
  423.1 1.0 convolution_bitcast_fusion
  424.1 0.7 fusion.32
  424.8 8.4 %fusion.1 = f32[]{:T(128)} fusion(bf16[8,512,768]{2,1,0:T(8,128)(2,1)} %res_ref.1, bf16[8,512,768]{2,1,0:T(8,128)(2,1)} %xg_ref.1), kind=kLoop, calls=%fused_computation.2 | loop fusion | flops 12582911 | bytes 12582916 | tf_op jit(solution)/shard_map/gsh,gsh->/dot_general | solution.py:509
  435.2 6.4 %copy-done = bf16[4,768,3072]{2,1,0:T(8,128)(2,1)S(1)} copy-done((bf16[4,768,3072]{2,1,0:T(8,128)(2,1)S(1)}, bf16[4,768,3072]{2,1,0:T(8,128)(2,1)}, u32[]{:S(2)}) %copy-start) | copy-done | bytes 18874392
  441.6 20.6 %settle.1 = (bf16[4,768,3072]{2,1,0:T(8,128)(2,1)}, bf16[4,3072,768]{2,1,0:T(8,128)(2,1)}) custom-call(bf16[4,768,3072]{2,1,0:T(8,128)(2,1)S(1)} %copy-done, bf16[4,3072,768]{2,1,0:T(8,128)(2,1)} %get-tuple-element.40.b_ref), custom_call_target="tpu_custom_call" | custom-call | flops 17179869184 | bytes 75497472 | tf_op jit(solution)/shard_map/settle/pallas_call | solution.py:425
  462.1 13.1 %all-to-all-done = bf16[16,256,768]{2,1,0:T(8,128)(2,1)} async-done(((bf16[16,256,768]{2,1,0:T(8,128)(2,1)}), bf16[16,256,768]{2,1,0:T(8,128)(2,1)}, u32[]{:S(2)}, u32[]{:S(2)}) %all-to-all-start) | async-done | bytes 6291488 | tf_op jit(solution)/shard_map/all_to_all | solution.py:493
  475.2 15.9 %all_reduce.1 = f32[16,32,128]{2,1,0:T(8,128)S(1)} custom-call(f32[16,32,128]{2,1,0:T(8,128)S(1)} %concatenate.7.part_ref), custom_call_target="tpu_custom_call" | custom-call | flops 4194304 | bytes 262144 | tf_op jit(solution)/shard_map/all_reduce/pallas_call | solution.py:462
  491.2 0.5 slice.21
  491.7 0.7 reshape.88
  492.4 14.9 %combine.1 = bf16[8,512,768]{2,1,0:T(8,128)(2,1)} custom-call(s32[8,1,512]{2,1,0:T(1,128)} %get-tuple-element.24.l1_ref, s32[8,1,512]{2,1,0:T(1,128)} %get-tuple-element.25.l2_ref, bf16[2,16,8,16,768]{4,3,2,1,0:T(8,128)(2,1)} %get-tuple-element.37.early_ref, bf16[16,2,8,16,768]{4,3,2,1,0:T(8,128)(2,1)} %bitcast.13.late_ref, bf16[8,512,768]{2,1,0:T(8,128)(2,1)} %res_ref.1, ...), custom_call_target="tpu_custom_call" | custom-call | flops 6442450944 | bytes 31457280 | tf_op jit(solution)/shard_map/combine/pallas_call | solution.py:399
  (19 shorter events, 0.1 us)
Async XLA Ops:
  390.7 3.5 copy-start.7
  390.7 3.7 copy-start.3
  390.7 84.5 %all-to-all-start = ((bf16[16,256,768]{2,1,0:T(8,128)(2,1)}), bf16[16,256,768]{2,1,0:T(8,128)(2,1)}, u32[]{:S(2)}, u32[]{:S(2)}) async-start(bf16[16,256,768]{2,1,0:T(8,128)(2,1)} %bitcast.44), calls=%async_computation | async-start | bytes 12582912 | tf_op jit(solution)/shard_map/all_to_all | solution.py:493
  399.0 2.0 copy-start.6
  399.0 3.6 copy-start.4
  399.1 3.6 copy-start.5
  406.3 16.8 %slice-start = ((s8[6291456]{0:T(1024)(128)(4,1)}), s8[4194304]{0:T(1024)(128)(4,1)S(1)}, s32[]{:S(2)}) async-start(s8[6291456]{0:T(1024)(128)(4,1)} %bitcast.42), calls=%async_computation.1 | async-start | bytes 8388608
  410.3 12.8 %slice-start.1 = ((s8[6291456]{0:T(1024)(128)(4,1)}), s8[2097152]{0:T(1024)(128)(4,1)S(1)}, s32[]{:S(2)}) async-start(s8[6291456]{0:T(1024)(128)(4,1)} %bitcast.42), calls=%async_computation.2 | async-start | bytes 4194304
  422.1 1.0 copy-start.1
  423.1 1.0 copy-start.2
  435.2 6.4 %copy-start = (bf16[4,768,3072]{2,1,0:T(8,128)(2,1)S(1)}, bf16[4,768,3072]{2,1,0:T(8,128)(2,1)}, u32[]{:S(2)}) copy-start(bf16[4,768,3072]{2,1,0:T(8,128)(2,1)} %get-tuple-element.39.a_ref) | copy-start | bytes 56623108
